TPU v7x, 256 devices: a whole 4x4x8 slice. The times are simulated.
256 devices in a mesh: rep: 2 (over y_hi), fsdp: 128 (over z, x, y_lo, core).
Axes of the slice: x: 4, y: 4 (y_hi: 2, y_lo: 2; y = y_hi * 2 + y_lo), z: 8, core: 2. Of those that a mesh axis runs over, the one named last changes fastest.
Arguments:
- tokens: bfloat16 [131072, 4096], P(('rep', 'fsdp')), may hold values from -24 to 24
- value_cot: bfloat16 [131072, 1024], P(('rep', 'fsdp')), may hold values from -6 to 6
- value_weight: bfloat16 [2, 4096, 1024], P('rep', 'fsdp'), may hold values from -0.09375 to 0.09375
- global_params: float32 [16777216], P('fsdp'), may hold values from -6 to 6
- local_params: float32 [2, 16777216], P('rep', 'fsdp'), may hold values from -6 to 6
- momentum: float32 [16777216], P('fsdp'), may hold values from -3 to 3
Outputs:
- token_grad: bfloat16 [131072, 4096], P(('rep', 'fsdp'))
- value_grad: float32 [2, 4096, 1024], P('rep', 'fsdp')
- new_global: float32 [16777216], P('fsdp')
- new_moment: float32 [16777216], P('fsdp')
All inputs are finite; a program needn't handle non-finite values.
Results may differ from a plain program's by a relative error of at most 0.001.
Values may be sent and summed in bfloat16 or wider, within the bound.
No kernel may reach another device: no remote copies, remote signals or barrier semaphores. Data moves between devices by JAX's collectives and lax.ppermute only.
A program may use at most 128 MiB of HBM per device.

v0:
```python
import functools

import jax
import jax.numpy as jnp
from jax import lax
from jax.experimental import pallas as pl
from jax.experimental.pallas import tpu as pltpu
from jax.sharding import Mesh
from jax.sharding import PartitionSpec as P


FSDP = ("z", "x", "y", "c")
REP_FSDP = ("rep", "z", "x", "y", "c")
NZ, NX = 8, 4
SWAP = [(0, 1), (1, 0)]
Z_STEP = [(2 * i + c, 2 * ((i + 1 - 2 * c) % NZ) + c) for i in range(NZ) for c in range(2)]
Z_UP = [(2 * i, 2 * ((i + 1) % NZ)) for i in range(NZ)]
X_STEP = [(2 * i + c, 2 * ((i + 1 - 2 * c) % NX) + c) for i in range(NX) for c in range(2)]
F32 = jnp.float32
DATA, TAIL = 128, 8
BLOCK = DATA + TAIL


def tall(value):
    return value.reshape(-1, BLOCK, value.shape[-1])


def with_tails(body, up):
    row = lax.broadcasted_iota(jnp.int32, body.shape, 1)
    return jnp.where(row < DATA, body, up)


def scale_row(value):
    return value[0:1, DATA : DATA + 1].astype(F32)


def fourth(v):
    return (v * v) * (v * v)


def combine(*parts):
    ups = [scale_row(p) for p in parts]
    up = functools.reduce(jnp.maximum, ups)
    inverse = 1.0 / up
    body = sum(p.astype(F32) * fourth(u * inverse) for p, u in zip(parts, ups))
    return with_tails(body, up)


def term_kernel(_, *refs):
    *cols, cot_a, cot_b, out = refs
    dims = (((0,), (0,)), ((), ()))
    mine = jnp.concatenate([r[...] for r in cols[:4]], axis=1)
    total = lax.dot_general(mine, cot_a[...], dims, preferred_element_type=F32)
    theirs = jnp.concatenate([r[...] for r in cols[4:]], axis=1)
    total += lax.dot_general(theirs, cot_b[...], dims, preferred_element_type=F32)
    top = jnp.full((TAIL, out.shape[-1]), jnp.maximum(jnp.max(jnp.abs(total)), 1e-30), F32)
    power = jnp.clip(jnp.ceil((jnp.log2(top) - 8.5) * 0.25), -14.0, 14.0)
    down = fourth(jnp.exp2(-power[:1]))
    up = jnp.exp2(power)
    for k in range(4):
        out[k * BLOCK : k * BLOCK + DATA, :] = total[k * DATA : (k + 1) * DATA] * down
        out[k * BLOCK + DATA : (k + 1) * BLOCK, :] = up


def grad_terms(chunks, tokens, cot, other_tokens, other_cot):
    rows, width = cot.shape
    count = len(chunks)
    ids = jnp.concatenate(chunks).astype(jnp.int32)
    spec = [pl.BlockSpec((rows, DATA), functools.partial(lambda k, i, ids: (0, ids[4 * i + k]), k)) for k in range(4)]
    whole = pl.BlockSpec((rows, width), lambda i, ids: (0, 0))
    call = pl.pallas_call(
        term_kernel,
        grid_spec=pltpu.PrefetchScalarGridSpec(
            num_scalar_prefetch=1,
            grid=(count,),
            in_specs=spec + spec + [whole, whole],
            out_specs=pl.BlockSpec((4 * BLOCK, width), lambda i, ids: (i, 0)),
        ),
        out_shape=jax.ShapeDtypeStruct((4 * BLOCK * count, width), F32),
        cost_estimate=pl.CostEstimate(
            flops=4 * rows * 512 * width * count, bytes_accessed=(2 + 3 * count) << 20, transcendentals=0
        ),
    )
    terms = call(ids, *[tokens] * 4, *[other_tokens] * 4, cot, other_cot)
    return [tall(terms[4 * BLOCK * k : 4 * BLOCK * (k + 1)]) for k in range(count)]


def sum_grad(tokens, cot, factor):
    z, x, y, c = (lax.axis_index(a) for a in FSDP)
    sign = 1 - 2 * c
    other_cot = lax.ppermute(cot, "c", SWAP)
    other_tokens = lax.ppermute(tokens, "c", SWAP)
    half = lambda v: v.astype(jnp.float16)
    steps = jnp.arange(4)
    up = (z + 4 - steps) % NZ
    down = jnp.where(steps == 0, z, z + 4 + steps) % NZ
    mine, theirs = jnp.where(c == 0, up, down), jnp.where(c == 0, down, up)
    near, far = (x + sign) % NX, (x + 2) % NX
    inputs = (tokens, cot, other_tokens, other_cot)
    (far_term,) = grad_terms([mine * NX + far], *inputs)
    from_far = lax.ppermute(half(far_term), ("x", "c"), X_STEP)
    cross, near_term, own_term = grad_terms([theirs * NX + near, mine * NX + near, mine * NX + x], *inputs)
    cross = half(cross)
    from_far, _ = lax.optimization_barrier((from_far, cross))
    cross = lax.ppermute(cross, ("x", "c"), X_STEP)
    cross = lax.ppermute(cross, "c", SWAP)
    direct = lax.ppermute(half(combine(near_term, from_far)), ("x", "c"), X_STEP)
    total = combine(own_term, cross, direct)
    came = lax.ppermute(half(total[0:1]), ("z", "c"), Z_UP)
    for k in range(1, 4):
        came = lax.ppermute(half(combine(total[k : k + 1], came)), ("z", "c"), Z_STEP)
    plain = lambda v: v[0, :DATA].astype(F32) * fourth(scale_row(v)[0])
    came = (plain(came) + jnp.where(c == 0, 0.0, plain(total[0:1]))).reshape(2, 2, 32, -1)
    pick = lambda v, i, dim: lax.dynamic_index_in_dim(v, i, dim, keepdims=False)
    rows = pick(came, c, 1) + lax.ppermute(pick(came, 1 - c, 1), "c", SWAP)
    return (pick(rows, y, 0) + lax.ppermute(pick(rows, 1 - y, 0), "y", SWAP)) * factor


def token_kernel(where, *refs, count, halves):
    cot, blocks, out = refs[0], refs[1 : 1 + count], refs[-1]
    x = where[4]

    def one(block, base):
        got = lax.dot_general(
            cot[...], block[...], (((1,), (1,)), ((), ())), preferred_element_type=F32
        ).astype(out.dtype)
        for k in range(block.shape[0] // 128):
            col = lax.rem(x + base + k, NX)
            out[:, pl.ds(pl.multiple_of(col * 128, 128), 128)] = got[:, k * 128 : (k + 1) * 128]

    if halves:
        for k in range(count):
            one(blocks[k], where[5 + k])
    else:
        for k in range(count):
            pl.when(pl.program_id(0) == k)(functools.partial(one, blocks[k], 0))


def token_part(where, cot, blocks, done, halves=False):
    rows, width = cot.shape
    count = len(blocks)
    full = lambda s: pl.BlockSpec(s, lambda i, w: (0, 0))
    extra = [] if done is None else [done]
    size = sum(b.shape[0] for b in blocks)
    where = jnp.stack([jnp.asarray(v, jnp.int32) for v in where])
    return pl.pallas_call(
        functools.partial(token_kernel, count=count, halves=halves),
        grid_spec=pltpu.PrefetchScalarGridSpec(
            num_scalar_prefetch=1,
            grid=(1 if halves else count,),
            in_specs=[full((rows, width))]
            + [full(b.shape) for b in blocks]
            + [pl.BlockSpec(memory_space=pl.ANY)] * len(extra),
            out_specs=pl.BlockSpec((rows, 512), lambda i, w: (0, w[i])),
        ),
        out_shape=jax.ShapeDtypeStruct((rows, 4096), jnp.bfloat16),
        input_output_aliases={2 + count: 0} if extra else {},
        cost_estimate=pl.CostEstimate(flops=2 * rows * size * width, bytes_accessed=4 << 20, transcendentals=0),
    )(where, cot, *blocks, *extra)


def token_grads(cot, weight):
    z, x, y, c = (lax.axis_index(a) for a in FSDP)
    sign = 1 - 2 * c
    ring = lambda step: [(i, (i + step) % NX) for i in range(NX)]
    other = lax.ppermute(weight, "y", SWAP)
    pair = jnp.where(y == 0, jnp.stack([weight, other]), jnp.stack([other, weight]))
    others = [lax.ppermute(pair, "x", ring(NX - k)) for k in (1, 2, 3)]
    mine = jnp.stack([pair, *others])
    theirs = lax.ppermute(mine, "c", SWAP)
    block = jnp.where(c == 0, jnp.stack([mine, theirs], 2), jnp.stack([theirs, mine], 2)).reshape(512, -1)
    near, swapped = [], []
    own = block
    for _ in range(1, 4):
        block = lax.ppermute(block, ("z", "c"), Z_STEP)
        near.append(block)
        swapped.append(lax.ppermute(block, "c", SWAP))
    block = lax.ppermute(lax.dynamic_slice_in_dim(block, 256 * c, 256, 0), ("z", "c"), Z_STEP)
    other = lax.ppermute(block, "c", SWAP)
    at = lambda k: (z + k * sign) % NZ
    grad = token_part((z, at(-1), at(1), 0, x), cot, [own, near[0], swapped[0]], None)
    grad = token_part((at(-2), at(2), at(-3), at(3), x), cot, [near[1], swapped[1], near[2], swapped[2]], grad)
    return token_part((at(4), 0, 0, 0, x, 2 * c, 2 - 2 * c), cot, [block, other], grad, halves=True)


def step(tokens, value_cot, value_weight, global_params, local_params, momentum):
    mine = local_params[0]
    totals = mine + lax.ppermute(mine, "rep", SWAP)
    factor = 1.0 / jnp.sqrt(jnp.float32(tokens.shape[0] * lax.axis_size(FSDP)))
    token_grad = token_grads(value_cot, value_weight[0])
    value_grad = sum_grad(tokens, value_cot, factor)[None]
    pseudo = global_params - totals / lax.axis_size("rep")
    new_moment = 0.9 * momentum + pseudo
    new_global = global_params - 0.7 * (pseudo + 0.9 * new_moment)
    return (token_grad, value_grad, new_global, new_moment)


def solution(mesh):
    split = Mesh(mesh.devices.reshape(mesh.shape["rep"], NZ, NX, 2, 2), REP_FSDP)
    return jax.shard_map(
        step,
        mesh=split,
        in_specs=(
            P(REP_FSDP, None),
            P(REP_FSDP, None),
            P("rep", FSDP, None),
            P(FSDP),
            P("rep", FSDP),
            P(FSDP),
        ),
        out_specs=(P(REP_FSDP, None), P("rep", FSDP, None), P(FSDP), P(FSDP)),
        check_vma=False,
    )
```

profile of v0, /device:TPU:16, one launch (start us, length us, event | category | flops | bytes accessed | tf_op | source)
XLA Modules:
  0.0 158.9 jit_solution(5873028174413747261)
XLA Ops:
  1.8 7.8 %collective-permute-done.14.refs_9_ = bf16[512,1024]{1,0:T(8,128)(2,1)S(1)} collective-permute-done((bf16[512,1024]{1,0:T(8,128)(2,1)}, bf16[512,1024]{1,0:T(8,128)(2,1)S(1)}, u32[]{:S(2)}, u32[]{:S(2)}) %collective-permute-start.14) | collective-permute-done | bytes 1048608 | tf_op jit(solution)/shard_map/ppermute | solution.py:91
  9.6 1.0 copy-done.1
  10.6 5.6 %shard_map.97 = f32[544,1024]{1,0:T(8,128)} custom-call(s32[4]{0:T(128)} %get-tuple-element.34._, bf16[512,4096]{1,0:T(8,128)(2,1)} %refs_3_.3, bf16[512,4096]{1,0:T(8,128)(2,1)} %refs_3_.3, bf16[512,4096]{1,0:T(8,128)(2,1)} %refs_3_.3, bf16[512,4096]{1,0:T(8,128)(2,1)} %refs_3_.3, bf16[512,4096]{1,0:T(8,128)(2,1)} %collective-permute-done.13.refs_4_.refs_5_.refs_6_.refs_7_, ...), custom_call_target="tpu_custom_call" | custom-call | flops 1073741824 | bytes 5242880 | tf_op jit(solution)/shard_map/pallas_call | solution.py:84
  16.2 2.8 %convert_element_type.71 = f16[544,1024]{1,0:T(8,128)(2,1)} convert(f32[544,1024]{1,0:T(8,128)} %shard_map.97) | non-fusion elementwise | flops 557056 | bytes 3342336 | tf_op jit(solution)/shard_map/convert_element_type | solution.py:93
  19.1 1.5 collective-permute-start.17
  21.1 9.5 %shard_map.96 = f32[1632,1024]{1,0:T(8,128)} custom-call(s32[12]{0:T(128)} %pad_add_fusion._, bf16[512,4096]{1,0:T(8,128)(2,1)} %refs_3_.3, bf16[512,4096]{1,0:T(8,128)(2,1)} %refs_3_.3, bf16[512,4096]{1,0:T(8,128)(2,1)} %refs_3_.3, bf16[512,4096]{1,0:T(8,128)(2,1)} %refs_3_.3, bf16[512,4096]{1,0:T(8,128)(2,1)} %collective-permute-done.13.refs_4_.refs_5_.refs_6_.refs_7_, ...), custom_call_target="tpu_custom_call" | custom-call | flops 3221225472 | bytes 11534336 | tf_op jit(solution)/shard_map/pallas_call | solution.py:84
  30.6 5.1 %fusion.28 = (f32[544,1024]{1,0:T(8,128)}, f32[544,1024]{1,0:T(8,128)S(1)}, f16[544,1024]{1,0:T(8,128)(2,1)S(1)}) fusion(f32[1632,1024]{1,0:T(8,128)} %shard_map.96), kind=kLoop, calls=%fused_computation.83 | loop fusion | flops 557056 | bytes 12255232 | tf_op jit(solution)/shard_map/slice | solution.py:85
  35.8 1.5 collective-permute-start.15
  37.3 1.6 select_convert_fusion
  38.9 1.2 collective-permute-start.18
  40.1 12.4 %collective-permute-done.15 = f16[4,136,1024]{2,1,0:T(8,128)(2,1)S(1)} collective-permute-done((f16[4,136,1024]{2,1,0:T(8,128)(2,1)S(1)}, f16[4,136,1024]{2,1,0:T(8,128)(2,1)S(1)}, u32[]{:S(2)}, u32[]{:S(2)}) %collective-permute-start.15) | collective-permute-done | bytes 1114144 | tf_op jit(solution)/shard_map/ppermute | solution.py:105
  52.5 1.3 collective-permute-start
  53.8 3.2 %collective-permute-done = bf16[32,1024]{1,0:T(8,128)(2,1)S(1)} collective-permute-done((bf16[32,1024]{1,0:T(8,128)(2,1)S(1)}, bf16[32,1024]{1,0:T(8,128)(2,1)S(1)}, u32[]{:S(2)}, u32[]{:S(2)}) %collective-permute-start) | collective-permute-done | bytes 65568 | tf_op jit(solution)/shard_map/ppermute | solution.py:166
  57.4 2.9 %collective-permute-start.1 = (bf16[2,32,1024]{2,1,0:T(8,128)(2,1)S(1)}, bf16[2,32,1024]{2,1,0:T(8,128)(2,1)S(1)}, u32[]{:S(2)}, u32[]{:S(2)}) collective-permute-start(bf16[2,32,1024]{2,1,0:T(8,128)(2,1)S(1)} %maximum_select_fusion.2), channel_id=1, source_target_pairs={{0,12},{4,0},{8,4},{12,8},{1,13},{5,1},{9,5},{13,9},{2,14},{6,2},{... | collective-permute-start | bytes 393224 | tf_op jit(solution)/shard_map/ppermute | solution.py:168
  60.6 8.0 %collective-permute-done.3 = bf16[2,32,1024]{2,1,0:T(8,128)(2,1)S(1)} collective-permute-done((bf16[2,32,1024]{2,1,0:T(8,128)(2,1)S(1)}, bf16[2,32,1024]{2,1,0:T(8,128)(2,1)S(1)}, u32[]{:S(2)}, u32[]{:S(2)}) %collective-permute-start.3) | collective-permute-done | bytes 131104 | tf_op jit(solution)/shard_map/ppermute | solution.py:168
  68.6 1.4 collective-permute-done.2
  70.2 1.9 %collective-permute-done.4 = bf16[4,2,32,1024]{3,2,1,0:T(8,128)(2,1)S(1)} collective-permute-done((bf16[4,2,32,1024]{3,2,1,0:T(8,128)(2,1)S(1)}, bf16[4,2,32,1024]{3,2,1,0:T(8,128)(2,1)S(1)}, u32[]{:S(2)}, u32[]{:S(2)}) %collective-permute-start.4) | collective-permute-done | bytes 524320 | tf_op jit(solution)/shard_map/ppermute | solution.py:170
  72.4 2.2 %collective-permute-start.5 = (bf16[512,1024]{1,0:T(8,128)(2,1)S(1)}, bf16[512,1024]{1,0:T(8,128)(2,1)S(1)}, u32[]{:S(2)}, u32[]{:S(2)}) collective-permute-start(bf16[512,1024]{1,0:T(8,128)(2,1)S(1)} %bitcast.66), channel_id=1, source_target_pairs={{0,16},{1,113},{16,32},{17,1},{32,48},{33,17},{48,64},{49,33},{64,... | collective-permute-start | bytes 3145736 | tf_op jit(solution)/shard_map/ppermute | solution.py:175
  76.1 2.3 %add_select_fusion = f32[4,136,1024]{2,1,0:T(8,128)S(1)} fusion(f16[4,136,1024]{2,1,0:T(8,128)(2,1)} %collective-permute-done.18, f16[4,136,1024]{2,1,0:T(8,128)(2,1)} %collective-permute-done.16, f32[4,136,1024]{2,1,0:T(8,128)S(1)} %bitcast.65, f32[1024]{0:T(1024)S(1)} %bitcast.96, f32[1024]{0:T(1024)S(1)} %bitcast.91, f32[1024]{0:T(1024)S(1)} %bitcast.90, ...), kind=kLoop, calls=%fused_computation.1 | loop fusion | flops 4456448 | bytes 6701192 | tf_op jit(solution)/shard_map/jit(_where)/select_n | solution.py:30
  78.5 3.8 %collective-permute-start.19 = (f16[1,136,1024]{2,1,0:T(8,128)(2,1)S(1)}, f16[1,136,1024]{2,1,0:T(8,128)(2,1)S(1)}, u32[]{:S(2)}, u32[]{:S(2)}) collective-permute-start(f16[1,136,1024]{2,1,0:T(8,128)(2,1)S(1)} %slice_convert_fusion.1), channel_id=1, source_target_pairs={{0,16},{16,32},{32,48},{48,64},{64,80},{80,96},{96,112},{112,0},{2... | collective-permute-start | bytes 835592 | tf_op jit(solution)/shard_map/ppermute | solution.py:109
  82.4 11.9 %collective-permute-done.19 = f16[1,136,1024]{2,1,0:T(8,128)(2,1)S(1)} collective-permute-done((f16[1,136,1024]{2,1,0:T(8,128)(2,1)S(1)}, f16[1,136,1024]{2,1,0:T(8,128)(2,1)S(1)}, u32[]{:S(2)}, u32[]{:S(2)}) %collective-permute-start.19) | collective-permute-done | bytes 278560 | tf_op jit(solution)/shard_map/ppermute | solution.py:109
  95.3 7.6 %collective-permute-done.20 = f16[1,136,1024]{2,1,0:T(8,128)(2,1)S(1)} collective-permute-done((f16[1,136,1024]{2,1,0:T(8,128)(2,1)S(1)}, f16[1,136,1024]{2,1,0:T(8,128)(2,1)S(1)}, u32[]{:S(2)}, u32[]{:S(2)}) %collective-permute-start.20) | collective-permute-done | bytes 278560 | tf_op jit(solution)/shard_map/ppermute | solution.py:111
  103.2 11.0 %collective-permute-done.6.refs_1_ = bf16[512,1024]{1,0:T(8,128)(2,1)} collective-permute-done((bf16[512,1024]{1,0:T(8,128)(2,1)S(1)}, bf16[512,1024]{1,0:T(8,128)(2,1)}, u32[]{:S(2)}, u32[]{:S(2)}) %collective-permute-start.6) | collective-permute-done | bytes 1048608 | tf_op jit(solution)/shard_map/ppermute | solution.py:175
  114.2 2.9 %collective-permute-done.21 = f16[1,136,1024]{2,1,0:T(8,128)(2,1)S(1)} collective-permute-done((f16[1,136,1024]{2,1,0:T(8,128)(2,1)S(1)}, f16[1,136,1024]{2,1,0:T(8,128)(2,1)S(1)}, u32[]{:S(2)}, u32[]{:S(2)}) %collective-permute-start.21) | collective-permute-done | bytes 278560 | tf_op jit(solution)/shard_map/ppermute | solution.py:111
  120.2 1.2 stack.93.where
  121.9 8.5 %collective-permute-done.7.refs_3_ = bf16[512,1024]{1,0:T(8,128)(2,1)S(1)} collective-permute-done((bf16[512,1024]{1,0:T(8,128)(2,1)}, bf16[512,1024]{1,0:T(8,128)(2,1)S(1)}, u32[]{:S(2)}, u32[]{:S(2)}) %collective-permute-start.7) | collective-permute-done | bytes 1048608 | tf_op jit(solution)/shard_map/ppermute | solution.py:175
  131.5 2.1 %collective-permute-done.22 = f16[1,136,1024]{2,1,0:T(8,128)(2,1)} collective-permute-done((f16[1,136,1024]{2,1,0:T(8,128)(2,1)S(1)}, f16[1,136,1024]{2,1,0:T(8,128)(2,1)}, u32[]{:S(2)}, u32[]{:S(2)}) %collective-permute-start.22) | collective-permute-done | bytes 278560 | tf_op jit(solution)/shard_map/ppermute | solution.py:111
  136.0 2.3 %multiply_subtract_fusion = (f32[131072]{0:T(1024)}, f32[131072]{0:T(1024)}) fusion(f32[131072]{0:T(1024)S(1)} %copy-done.6, f32[131072]{0:T(1024)} %bitcast.50, f32[131072]{0:T(1024)} %collective-permute-done.25, f32[131072]{0:T(1024)S(1)} %copy-done.7), kind=kLoop, calls=%fused_computation.20 | loop fusion | flops 1179648 | bytes 3145728 | tf_op jit(solution)/shard_map/sub | solution.py:194
  138.4 6.1 %shard_map.93.refs_5_ = bf16[512,4096]{1,0:T(8,128)(2,1)} custom-call(s32[5]{0:T(128)} %stack.117.where, bf16[512,1024]{1,0:T(8,128)(2,1)} %refs_8_.3, bf16[512,1024]{1,0:T(8,128)(2,1)} %bitcast.67, bf16[512,1024]{1,0:T(8,128)(2,1)} %copy-done.4, bf16[512,1024]{1,0:T(8,128)(2,1)} %collective-permute-done.12.refs_3_), custom_call_target="tpu_custom_call" | custom-call | flops 1610612736 | bytes 4194304 | tf_op jit(solution)/shard_map/pallas_call | solution.py:146
  144.6 1.6 %collective-permute-start.24 = (f32[32,1024]{1,0:T(8,128)S(1)}, f32[32,1024]{1,0:T(8,128)S(1)}, u32[]{:S(2)}, u32[]{:S(2)}) collective-permute-start(f32[32,1024]{1,0:T(8,128)S(1)} %dynamic-slice_bitcast_fusion.1), channel_id=1, source_target_pairs={{0,2},{2,0},{1,3},{3,1},{4,6},{6,4},{5,7},{7,5},{8,10},{10,8},{9,1... | collective-permute-start | bytes 393224 | tf_op jit(solution)/shard_map/ppermute | solution.py:116
  147.2 7.3 %shard_map.94.refs_3_ = bf16[512,4096]{1,0:T(8,128)(2,1)} custom-call(s32[5]{0:T(128)} %stack.113.where, bf16[512,1024]{1,0:T(8,128)(2,1)} %refs_8_.3, bf16[512,1024]{1,0:T(8,128)(2,1)} %collective-permute-done.6.refs_1_, bf16[512,1024]{1,0:T(8,128)(2,1)} %collective-permute-done.10.refs_2_, ...), custom_call_target="tpu_custom_call", output_to_operand_aliasing={{}: (6, {})} | custom-call | flops 2147483648 | bytes 4194304 | tf_op jit(solution)/shard_map/pallas_call | solution.py:146
  154.5 3.7 %shard_map.95 = bf16[512,4096]{1,0:T(8,128)(2,1)} custom-call(s32[7]{0:T(128)} %stack.93.where, bf16[512,1024]{1,0:T(8,128)(2,1)} %refs_8_.3, bf16[256,1024]{1,0:T(8,128)(2,1)} %collective-permute-done.8.refs_1_, bf16[256,1024]{1,0:T(8,128)(2,1)} %collective-permute-done.9.refs_2_, bf16[512,4096]{1,0:T(8,128)(2,1)} %shard_map.94.refs_3_), custom_call_target="tpu_custom_call", output_to_operand_aliasing={{}: (4, {})} | custom-call | flops 536870912 | bytes 4194304 | tf_op jit(solution)/shard_map/pallas_call | solution.py:146
  (89 shorter events, 14.4 us)
Async XLA Ops:
  0.6 9.0 %collective-permute-start.13 = (bf16[512,4096]{1,0:T(8,128)(2,1)}, bf16[512,4096]{1,0:T(8,128)(2,1)}, u32[]{:S(2)}, u32[]{:S(2)}) collective-permute-start(bf16[512,4096]{1,0:T(8,128)(2,1)} %refs_3_.3), channel_id=1, source_target_pairs={{0,1},{1,0},{2,3},{3,2},{4,5},{5,4},{6,7},{7,6},{8,9},{9,8},{10,11... | collective-permute-start | bytes 12582920 | tf_op jit(solution)/shard_map/ppermute | solution.py:92
  0.7 8.9 %collective-permute-start.14 = (bf16[512,1024]{1,0:T(8,128)(2,1)}, bf16[512,1024]{1,0:T(8,128)(2,1)S(1)}, u32[]{:S(2)}, u32[]{:S(2)}) collective-permute-start(bf16[512,1024]{1,0:T(8,128)(2,1)} %refs_8_.3), channel_id=1, source_target_pairs={{0,1},{1,0},{2,3},{3,2},{4,5},{5,4},{6,7},{7,6},{8,9},{9,8},{10,11... | collective-permute-start | bytes 3145736 | tf_op jit(solution)/shard_map/ppermute | solution.py:91
  19.1 18.2 %collective-permute-start.17 = (f16[4,136,1024]{2,1,0:T(8,128)(2,1)}, f16[4,136,1024]{2,1,0:T(8,128)(2,1)S(1)}, u32[]{:S(2)}, u32[]{:S(2)}) collective-permute-start(f16[4,136,1024]{2,1,0:T(8,128)(2,1)} %bitcast.24), channel_id=1, source_target_pairs={{0,4},{1,13},{4,8},{5,1},{8,12},{9,5},{12,0},{13,9},{2,6},{3,15},{... | collective-permute-start | bytes 3342344 | tf_op jit(solution)/shard_map/ppermute | solution.py:101
  35.8 16.7 %collective-permute-start.15 = (f16[4,136,1024]{2,1,0:T(8,128)(2,1)S(1)}, f16[4,136,1024]{2,1,0:T(8,128)(2,1)S(1)}, u32[]{:S(2)}, u32[]{:S(2)}) collective-permute-start(f16[4,136,1024]{2,1,0:T(8,128)(2,1)S(1)} %bitcast.69), channel_id=1, source_target_pairs={{0,4},{1,13},{4,8},{5,1},{8,12},{9,5},{12,0},{13,9},{2,6},{3,15},{... | collective-permute-start | bytes 3342344 | tf_op jit(solution)/shard_map/ppermute | solution.py:105
  37.3 65.7 %copy-start.10 = (pred[136]{0:T(512)(128)(4,1)}, pred[136]{0:T(512)(128)(4,1)S(1)}, u32[]{:S(2)}) copy-start(pred[136]{0:T(512)(128)(4,1)S(1)} %iota_compare_fusion) | copy-start | bytes 412
  37.3 15.2 %copy-start.8 = (bf16[1,32,1024]{2,1,0:T(8,128)(2,1)S(1)}, bf16[1,32,1024]{2,1,0:T(8,128)(2,1)}, u32[]{:S(2)}) copy-start(bf16[1,32,1024]{2,1,0:T(8,128)(2,1)} %param.8) | copy-start | bytes 196612
  38.9 35.7 %collective-permute-start.18 = (f16[4,136,1024]{2,1,0:T(8,128)(2,1)}, f16[4,136,1024]{2,1,0:T(8,128)(2,1)}, u32[]{:S(2)}, u32[]{:S(2)}) collective-permute-start(f16[4,136,1024]{2,1,0:T(8,128)(2,1)} %select_convert_fusion), channel_id=1, source_target_pairs={{0,4},{1,13},{4,8},{5,1},{8,12},{9,5},{12,0},{13,9},{2,6},{3,15},{... | collective-permute-start | bytes 3342344 | tf_op jit(solution)/shard_map/ppermute | solution.py:107
  52.5 22.1 %collective-permute-start.16 = (f16[4,136,1024]{2,1,0:T(8,128)(2,1)S(1)}, f16[4,136,1024]{2,1,0:T(8,128)(2,1)}, u32[]{:S(2)}, u32[]{:S(2)}) collective-permute-start(f16[4,136,1024]{2,1,0:T(8,128)(2,1)S(1)} %collective-permute-done.15), channel_id=1, source_target_pairs={{0,1},{1,0},{2,3},{3,2},{4,5},{5,4},{6,7},{7,6},{8,9},{9,8},{10,11... | collective-permute-start | bytes 3342344 | tf_op jit(solution)/shard_map/ppermute | solution.py:106
  52.5 4.5 %collective-permute-start = (bf16[32,1024]{1,0:T(8,128)(2,1)S(1)}, bf16[32,1024]{1,0:T(8,128)(2,1)S(1)}, u32[]{:S(2)}, u32[]{:S(2)}) collective-permute-start(bf16[32,1024]{1,0:T(8,128)(2,1)S(1)} %bitcast.72), channel_id=1, source_target_pairs={{0,2},{2,0},{1,3},{3,1},{4,6},{6,4},{5,7},{7,5},{8,10},{10,8},{9,1... | collective-permute-start | bytes 196616 | tf_op jit(solution)/shard_map/ppermute | solution.py:166
  57.0 11.6 %collective-permute-start.3 = (bf16[2,32,1024]{2,1,0:T(8,128)(2,1)S(1)}, bf16[2,32,1024]{2,1,0:T(8,128)(2,1)S(1)}, u32[]{:S(2)}, u32[]{:S(2)}) collective-permute-start(bf16[2,32,1024]{2,1,0:T(8,128)(2,1)S(1)} %maximum_select_fusion.2), channel_id=1, source_target_pairs={{0,4},{4,8},{8,12},{12,0},{1,5},{5,9},{9,13},{13,1},{2,6},{6,10},{... | collective-permute-start | bytes 393224 | tf_op jit(solution)/shard_map/ppermute | solution.py:168
  57.4 11.3 %collective-permute-start.1 = (bf16[2,32,1024]{2,1,0:T(8,128)(2,1)S(1)}, bf16[2,32,1024]{2,1,0:T(8,128)(2,1)S(1)}, u32[]{:S(2)}, u32[]{:S(2)}) collective-permute-start(bf16[2,32,1024]{2,1,0:T(8,128)(2,1)S(1)} %maximum_select_fusion.2), channel_id=1, source_target_pairs={{0,12},{4,0},{8,4},{12,8},{1,13},{5,1},{9,5},{13,9},{2,14},{6,2},{... | collective-permute-start | bytes 393224 | tf_op jit(solution)/shard_map/ppermute | solution.py:168
  60.3 9.7 %collective-permute-start.2 = (bf16[2,32,1024]{2,1,0:T(8,128)(2,1)S(1)}, bf16[2,32,1024]{2,1,0:T(8,128)(2,1)S(1)}, u32[]{:S(2)}, u32[]{:S(2)}) collective-permute-start(bf16[2,32,1024]{2,1,0:T(8,128)(2,1)S(1)} %maximum_select_fusion.2), channel_id=1, source_target_pairs={{0,8},{4,12},{8,0},{12,4},{1,9},{5,13},{9,1},{13,5},{2,10},{6,14},... | collective-permute-start | bytes 393224 | tf_op jit(solution)/shard_map/ppermute | solution.py:168
  70.1 2.0 %collective-permute-start.4 = (bf16[4,2,32,1024]{3,2,1,0:T(8,128)(2,1)S(1)}, bf16[4,2,32,1024]{3,2,1,0:T(8,128)(2,1)S(1)}, u32[]{:S(2)}, u32[]{:S(2)}) collective-permute-start(bf16[4,2,32,1024]{3,2,1,0:T(8,128)(2,1)S(1)} %get-tuple-element.30), channel_id=1, source_target_pairs={{0,1},{1,0},{2,3},{3,2},{4,5},{5,4},{6,7},{7,6},{8,9},{9,8},{10,11... | collective-permute-start | bytes 1572872 | tf_op jit(solution)/shard_map/ppermute | solution.py:170
  72.4 22.7 %collective-permute-start.5 = (bf16[512,1024]{1,0:T(8,128)(2,1)S(1)}, bf16[512,1024]{1,0:T(8,128)(2,1)S(1)}, u32[]{:S(2)}, u32[]{:S(2)}) collective-permute-start(bf16[512,1024]{1,0:T(8,128)(2,1)S(1)} %bitcast.66), channel_id=1, source_target_pairs={{0,16},{1,113},{16,32},{17,1},{32,48},{33,17},{48,64},{49,33},{64,... | collective-permute-start | bytes 3145736 | tf_op jit(solution)/shard_map/ppermute | solution.py:175
  78.5 15.8 %collective-permute-start.19 = (f16[1,136,1024]{2,1,0:T(8,128)(2,1)S(1)}, f16[1,136,1024]{2,1,0:T(8,128)(2,1)S(1)}, u32[]{:S(2)}, u32[]{:S(2)}) collective-permute-start(f16[1,136,1024]{2,1,0:T(8,128)(2,1)S(1)} %slice_convert_fusion.1), channel_id=1, source_target_pairs={{0,16},{16,32},{32,48},{48,64},{64,80},{80,96},{96,112},{112,0},{2... | collective-permute-start | bytes 835592 | tf_op jit(solution)/shard_map/ppermute | solution.py:109
  95.1 7.8 %collective-permute-start.20 = (f16[1,136,1024]{2,1,0:T(8,128)(2,1)S(1)}, f16[1,136,1024]{2,1,0:T(8,128)(2,1)S(1)}, u32[]{:S(2)}, u32[]{:S(2)}) collective-permute-start(f16[1,136,1024]{2,1,0:T(8,128)(2,1)S(1)} %fusion.2), channel_id=1, source_target_pairs={{0,16},{1,113},{16,32},{17,1},{32,48},{33,17},{48,64},{49,33},{64,... | collective-permute-start | bytes 835592 | tf_op jit(solution)/shard_map/ppermute | solution.py:111
  95.2 8.0 %copy-start.4 = (bf16[512,1024]{1,0:T(8,128)(2,1)}, bf16[512,1024]{1,0:T(8,128)(2,1)S(1)}, u32[]{:S(2)}) copy-start(bf16[512,1024]{1,0:T(8,128)(2,1)S(1)} %collective-permute-done.5.refs_2_) | copy-start | bytes 3145732
  95.2 19.1 %collective-permute-start.6 = (bf16[512,1024]{1,0:T(8,128)(2,1)S(1)}, bf16[512,1024]{1,0:T(8,128)(2,1)}, u32[]{:S(2)}, u32[]{:S(2)}) collective-permute-start(bf16[512,1024]{1,0:T(8,128)(2,1)S(1)} %collective-permute-done.5.refs_2_), channel_id=1, source_target_pairs={{0,16},{1,113},{16,32},{17,1},{32,48},{33,17},{48,64},{49,33},{64,... | collective-permute-start | bytes 3145736 | tf_op jit(solution)/shard_map/ppermute | solution.py:175
  103.1 14.0 %collective-permute-start.21 = (f16[1,136,1024]{2,1,0:T(8,128)(2,1)S(1)}, f16[1,136,1024]{2,1,0:T(8,128)(2,1)S(1)}, u32[]{:S(2)}, u32[]{:S(2)}) collective-permute-start(f16[1,136,1024]{2,1,0:T(8,128)(2,1)S(1)} %fusion.5), channel_id=1, source_target_pairs={{0,16},{1,113},{16,32},{17,1},{32,48},{33,17},{48,64},{49,33},{64,... | collective-permute-start | bytes 835592 | tf_op jit(solution)/shard_map/ppermute | solution.py:111
  114.2 16.2 %collective-permute-start.7 = (bf16[512,1024]{1,0:T(8,128)(2,1)}, bf16[512,1024]{1,0:T(8,128)(2,1)S(1)}, u32[]{:S(2)}, u32[]{:S(2)}) collective-permute-start(bf16[512,1024]{1,0:T(8,128)(2,1)} %collective-permute-done.6.refs_1_), channel_id=1, source_target_pairs={{0,16},{1,113},{16,32},{17,1},{32,48},{33,17},{48,64},{49,33},{64,... | collective-permute-start | bytes 3145736 | tf_op jit(solution)/shard_map/ppermute | solution.py:175
  117.9 15.6 %collective-permute-start.22 = (f16[1,136,1024]{2,1,0:T(8,128)(2,1)S(1)}, f16[1,136,1024]{2,1,0:T(8,128)(2,1)}, u32[]{:S(2)}, u32[]{:S(2)}) collective-permute-start(f16[1,136,1024]{2,1,0:T(8,128)(2,1)S(1)} %fusion.8), channel_id=1, source_target_pairs={{0,16},{1,113},{16,32},{17,1},{32,48},{33,17},{48,64},{49,33},{64,... | collective-permute-start | bytes 835592 | tf_op jit(solution)/shard_map/ppermute | solution.py:111
  118.0 17.4 %collective-permute-start.25 = (f32[131072]{0:T(1024)}, f32[131072]{0:T(1024)}, u32[]{:S(2)}, u32[]{:S(2)}) collective-permute-start(f32[131072]{0:T(1024)} %bitcast.50), channel_id=1, source_target_pairs={{0,128},{128,0},{1,129},{129,1},{2,130},{130,2},{3,131},{131,3},{4... | collective-permute-start | bytes 1572872 | tf_op jit(solution)/shard_map/ppermute | solution.py:188
  121.4 13.9 %copy-start.9 = (f32[1,1,1024]{2,1,0:T(1,128)S(1)}, f32[1,1,1024]{2,1,0:T(1,128)}, u32[]{:S(2)}) copy-start(f32[1,1,1024]{2,1,0:T(1,128)} %get-tuple-element.28) | copy-start | bytes 12292
  121.4 14.6 %copy-start.6 = (f32[131072]{0:T(1024)S(1)}, f32[131072]{0:T(1024)}, u32[]{:S(2)}) copy-start(f32[131072]{0:T(1024)} %param.9) | copy-start | bytes 1572868
  121.4 14.6 %copy-start.7 = (f32[131072]{0:T(1024)S(1)}, f32[131072]{0:T(1024)}, u32[]{:S(2)}) copy-start(f32[131072]{0:T(1024)} %param.11) | copy-start | bytes 1572868
  121.4 17.0 %collective-permute-start.12 = (bf16[512,1024]{1,0:T(8,128)(2,1)}, bf16[512,1024]{1,0:T(8,128)(2,1)}, u32[]{:S(2)}, u32[]{:S(2)}) collective-permute-start(bf16[512,1024]{1,0:T(8,128)(2,1)} %copy-done.4), channel_id=1, source_target_pairs={{0,1},{1,0},{2,3},{3,2},{4,5},{5,4},{6,7},{7,6},{8,9},{9,8},{10,11... | collective-permute-start | bytes 3145736 | tf_op jit(solution)/shard_map/ppermute | solution.py:177
  121.4 24.8 %collective-permute-start.10 = (bf16[512,1024]{1,0:T(8,128)(2,1)}, bf16[512,1024]{1,0:T(8,128)(2,1)}, u32[]{:S(2)}, u32[]{:S(2)}) collective-permute-start(bf16[512,1024]{1,0:T(8,128)(2,1)} %collective-permute-done.6.refs_1_), channel_id=1, source_target_pairs={{0,1},{1,0},{2,3},{3,2},{4,5},{5,4},{6,7},{7,6},{8,9},{9,8},{10,11... | collective-permute-start | bytes 3145736 | tf_op jit(solution)/shard_map/ppermute | solution.py:177
  131.4 13.1 %collective-permute-start.8 = (bf16[256,1024]{1,0:T(8,128)(2,1)}, bf16[256,1024]{1,0:T(8,128)(2,1)}, u32[]{:S(2)}, u32[]{:S(2)}) collective-permute-start(bf16[256,1024]{1,0:T(8,128)(2,1)} %constant_dynamic-slice_fusion), channel_id=1, source_target_pairs={{0,16},{1,113},{16,32},{17,1},{32,48},{33,17},{48,64},{49,33},{64,... | collective-permute-start | bytes 1572872 | tf_op jit(solution)/shard_map/ppermute | solution.py:178
  133.5 12.6 %collective-permute-start.11 = (bf16[512,1024]{1,0:T(8,128)(2,1)S(1)}, bf16[512,1024]{1,0:T(8,128)(2,1)S(1)}, u32[]{:S(2)}, u32[]{:S(2)}) collective-permute-start(bf16[512,1024]{1,0:T(8,128)(2,1)S(1)} %collective-permute-done.7.refs_3_), channel_id=1, source_target_pairs={{0,1},{1,0},{2,3},{3,2},{4,5},{5,4},{6,7},{7,6},{8,9},{9,8},{10,11... | collective-permute-start | bytes 3145736 | tf_op jit(solution)/shard_map/ppermute | solution.py:177
  135.4 9.1 %collective-permute-start.23 = (f32[2,32,1024]{2,1,0:T(8,128)S(1)}, f32[2,32,1024]{2,1,0:T(8,128)S(1)}, u32[]{:S(2)}, u32[]{:S(2)}) collective-permute-start(f32[2,32,1024]{2,1,0:T(8,128)S(1)} %dynamic-slice_bitcast_fusion), channel_id=1, source_target_pairs={{0,1},{1,0},{2,3},{3,2},{4,5},{5,4},{6,7},{7,6},{8,9},{9,8},{10,11... | collective-permute-start | bytes 786440 | tf_op jit(solution)/shard_map/ppermute | solution.py:115
  144.5 10.0 %collective-permute-start.9 = (bf16[256,1024]{1,0:T(8,128)(2,1)}, bf16[256,1024]{1,0:T(8,128)(2,1)}, u32[]{:S(2)}, u32[]{:S(2)}) collective-permute-start(bf16[256,1024]{1,0:T(8,128)(2,1)} %collective-permute-done.8.refs_1_), channel_id=1, source_target_pairs={{0,1},{1,0},{2,3},{3,2},{4,5},{5,4},{6,7},{7,6},{8,9},{9,8},{10,11... | collective-permute-start | bytes 1572872 | tf_op jit(solution)/shard_map/ppermute | solution.py:179
  144.6 13.6 %collective-permute-start.24 = (f32[32,1024]{1,0:T(8,128)S(1)}, f32[32,1024]{1,0:T(8,128)S(1)}, u32[]{:S(2)}, u32[]{:S(2)}) collective-permute-start(f32[32,1024]{1,0:T(8,128)S(1)} %dynamic-slice_bitcast_fusion.1), channel_id=1, source_target_pairs={{0,2},{2,0},{1,3},{3,1},{4,6},{6,4},{5,7},{7,5},{8,10},{10,8},{9,1... | collective-permute-start | bytes 393224 | tf_op jit(solution)/shard_map/ppermute | solution.py:116
  (5 other events, 17.6 us)
where the time goes:
time: 161 us; the launch traced here: 159 us
  waiting for transfers between devices  78.8 us (49%)
  Pallas kernels  32.2 us (20%)
  other arithmetic  20.5 us (13%)
  starting transfers between devices  19.3 us (12%)
  local copies, waits for them, and re-layouts  7.18 us (4%)
    ppermute x3, waiting for transfers between devices, token_grads(): block = lax.ppermute(block, ('z', 'c'), Z_STEP)  19.6 us
    pallas_call x3, Pallas kernels, token_part(): pl.pallas_call(functools.partial(token_kernel, count=count, halves=halves...  17.2 us
    pallas_call x2, Pallas kernels, grad_terms(): terms = call(ids, *[tokens] * 4, *[other_tokens] * 4, cot, other_cot)  15.1 us
    ppermute x3, waiting for transfers between devices, sum_grad(): came = lax.ppermute(half(combine(total[k:k + 1], came)), ('z', 'c'), Z_STEP)  12.6 us
    ppermute x1, waiting for transfers between devices, sum_grad(): cross = lax.ppermute(cross, ('x', 'c'), X_STEP)  12.4 us
    ppermute x1, waiting for transfers between devices, sum_grad(): came = lax.ppermute(half(total[0:1]), ('z', 'c'), Z_UP)  11.9 us
    ppermute x3, waiting for transfers between devices, token_grads(): others = [lax.ppermute(pair, 'x', ring(NX - k)) for k in (1, 2, 3)]  9.38 us
    ppermute x1, waiting for transfers between devices, sum_grad(): other_cot = lax.ppermute(cot, 'c', SWAP)  7.8 us
  transfers between devices with their start and end apart: 26, of which 12 were waited for; matrix products, arithmetic and copies ran while one was open for 14% of the time, Pallas kernels for 17%

commit v1 on v0

--- a/solution.py
+++ b/solution.py
@@ -14,7 +14,7 @@
 NZ, NX = 8, 4
 SWAP = [(0, 1), (1, 0)]
 Z_STEP = [(2 * i + c, 2 * ((i + 1 - 2 * c) % NZ) + c) for i in range(NZ) for c in range(2)]
-Z_UP = [(2 * i, 2 * ((i + 1) % NZ)) for i in range(NZ)]
+Z_FAR = [(2 * i, 2 * ((i + 4) % NZ)) for i in range(NZ)]
 X_STEP = [(2 * i + c, 2 * ((i + 1 - 2 * c) % NX) + c) for i in range(NX) for c in range(2)]
 F32 = jnp.float32
 DATA, TAIL = 128, 8
@@ -25,13 +25,14 @@
     return value.reshape(-1, BLOCK, value.shape[-1])
 
 
-def with_tails(body, up):
+def with_tails(body, up, down):
     row = lax.broadcasted_iota(jnp.int32, body.shape, 1)
-    return jnp.where(row < DATA, body, up)
-
-
-def scale_row(value):
-    return value[0:1, DATA : DATA + 1].astype(F32)
+    return jnp.where(row < DATA, body, jnp.where(row < DATA + TAIL // 2, up, down))
+
+
+def scale_rows(value):
+    low = DATA + TAIL // 2
+    return value[0:1, DATA : DATA + 1].astype(F32), value[0:1, low : low + 1].astype(F32)
 
 
 def fourth(v):
@@ -39,49 +40,73 @@
 
 
 def combine(*parts):
-    ups = [scale_row(p) for p in parts]
+    ups, downs = zip(*[scale_rows(p) for p in parts])
     up = functools.reduce(jnp.maximum, ups)
-    inverse = 1.0 / up
-    body = sum(p.astype(F32) * fourth(u * inverse) for p, u in zip(parts, ups))
-    return with_tails(body, up)
+    down = functools.reduce(jnp.minimum, downs)
+    body = sum(p.astype(F32) * fourth(u * down) for p, u in zip(parts, ups))
+    return with_tails(body, up, down)
+
+
+def pick_kernel(_, *refs):
+    refs[-1][0] = jnp.concatenate([r[...] for r in refs[:4]], axis=1)
+
+
+def column_specs(rows):
+    return [pl.BlockSpec((rows, DATA), functools.partial(lambda k, i, ids: (0, ids[4 * i + k]), k)) for k in range(4)]
+
+
+def pick_columns(chunks, tokens):
+    rows = tokens.shape[0]
+    count = len(chunks)
+    return pl.pallas_call(
+        pick_kernel,
+        grid_spec=pltpu.PrefetchScalarGridSpec(
+            num_scalar_prefetch=1,
+            grid=(count,),
+            in_specs=column_specs(rows),
+            out_specs=pl.BlockSpec((1, rows, 512), lambda i, ids: (i, 0, 0)),
+        ),
+        out_shape=jax.ShapeDtypeStruct((count, rows, 512), tokens.dtype),
+        compiler_params=pltpu.CompilerParams(vmem_limit_bytes=16 << 20),
+        cost_estimate=pl.CostEstimate(flops=rows * 512 * count, bytes_accessed=count << 20, transcendentals=0),
+    )(jnp.concatenate(chunks).astype(jnp.int32), *[tokens] * 4)
 
 
 def term_kernel(_, *refs):
-    *cols, cot_a, cot_b, out = refs
+    *cols, theirs, cot_a, cot_b, out = refs
     dims = (((0,), (0,)), ((), ()))
-    mine = jnp.concatenate([r[...] for r in cols[:4]], axis=1)
+    mine = jnp.concatenate([r[...] for r in cols], axis=1)
     total = lax.dot_general(mine, cot_a[...], dims, preferred_element_type=F32)
-    theirs = jnp.concatenate([r[...] for r in cols[4:]], axis=1)
-    total += lax.dot_general(theirs, cot_b[...], dims, preferred_element_type=F32)
+    total += lax.dot_general(theirs[0], cot_b[...], dims, preferred_element_type=F32)
     top = jnp.full((TAIL, out.shape[-1]), jnp.maximum(jnp.max(jnp.abs(total)), 1e-30), F32)
     power = jnp.clip(jnp.ceil((jnp.log2(top) - 8.5) * 0.25), -14.0, 14.0)
     down = fourth(jnp.exp2(-power[:1]))
-    up = jnp.exp2(power)
+    row = lax.broadcasted_iota(jnp.int32, power.shape, 0)
+    tail = jnp.exp2(jnp.where(row < TAIL // 2, power, -power))
     for k in range(4):
         out[k * BLOCK : k * BLOCK + DATA, :] = total[k * DATA : (k + 1) * DATA] * down
-        out[k * BLOCK + DATA : (k + 1) * BLOCK, :] = up
-
-
-def grad_terms(chunks, tokens, cot, other_tokens, other_cot):
+        out[k * BLOCK + DATA : (k + 1) * BLOCK, :] = tail
+
+
+def grad_terms(chunks, tokens, cot, others, other_cot):
     rows, width = cot.shape
     count = len(chunks)
-    ids = jnp.concatenate(chunks).astype(jnp.int32)
-    spec = [pl.BlockSpec((rows, DATA), functools.partial(lambda k, i, ids: (0, ids[4 * i + k]), k)) for k in range(4)]
     whole = pl.BlockSpec((rows, width), lambda i, ids: (0, 0))
     call = pl.pallas_call(
         term_kernel,
         grid_spec=pltpu.PrefetchScalarGridSpec(
             num_scalar_prefetch=1,
             grid=(count,),
-            in_specs=spec + spec + [whole, whole],
+            in_specs=column_specs(rows) + [pl.BlockSpec((1, rows, 512), lambda i, ids: (i, 0, 0)), whole, whole],
             out_specs=pl.BlockSpec((4 * BLOCK, width), lambda i, ids: (i, 0)),
         ),
         out_shape=jax.ShapeDtypeStruct((4 * BLOCK * count, width), F32),
+        compiler_params=pltpu.CompilerParams(vmem_limit_bytes=28 << 20),
         cost_estimate=pl.CostEstimate(
             flops=4 * rows * 512 * width * count, bytes_accessed=(2 + 3 * count) << 20, transcendentals=0
         ),
     )
-    terms = call(ids, *[tokens] * 4, *[other_tokens] * 4, cot, other_cot)
+    terms = call(jnp.concatenate(chunks).astype(jnp.int32), *[tokens] * 4, others, cot, other_cot)
     return [tall(terms[4 * BLOCK * k : 4 * BLOCK * (k + 1)]) for k in range(count)]
 
 
@@ -89,28 +114,36 @@
     z, x, y, c = (lax.axis_index(a) for a in FSDP)
     sign = 1 - 2 * c
     other_cot = lax.ppermute(cot, "c", SWAP)
-    other_tokens = lax.ppermute(tokens, "c", SWAP)
     half = lambda v: v.astype(jnp.float16)
     steps = jnp.arange(4)
     up = (z + 4 - steps) % NZ
     down = jnp.where(steps == 0, z, z + 4 + steps) % NZ
     mine, theirs = jnp.where(c == 0, up, down), jnp.where(c == 0, down, up)
     near, far = (x + sign) % NX, (x + 2) % NX
-    inputs = (tokens, cot, other_tokens, other_cot)
-    (far_term,) = grad_terms([mine * NX + far], *inputs)
+    away = (x - sign) % NX
+    first = pick_columns([theirs * NX + far], tokens)
+    rest = pick_columns([mine * NX + away, theirs * NX + away, theirs * NX + x], tokens)
+    first = lax.ppermute(first, "c", SWAP)
+    rest = lax.ppermute(rest, "c", SWAP)
+    (far_term,) = grad_terms([mine * NX + far], tokens, cot, first, other_cot)
     from_far = lax.ppermute(half(far_term), ("x", "c"), X_STEP)
-    cross, near_term, own_term = grad_terms([theirs * NX + near, mine * NX + near, mine * NX + x], *inputs)
+    cross, near_term, own_term = grad_terms(
+        [theirs * NX + near, mine * NX + near, mine * NX + x], tokens, cot, rest, other_cot
+    )
     cross = half(cross)
     from_far, _ = lax.optimization_barrier((from_far, cross))
     cross = lax.ppermute(cross, ("x", "c"), X_STEP)
     cross = lax.ppermute(cross, "c", SWAP)
     direct = lax.ppermute(half(combine(near_term, from_far)), ("x", "c"), X_STEP)
     total = combine(own_term, cross, direct)
-    came = lax.ppermute(half(total[0:1]), ("z", "c"), Z_UP)
+    straight = lax.ppermute(half(total[0:1]), ("z", "c"), Z_FAR)
+    came = half(total[1:2])
     for k in range(1, 4):
-        came = lax.ppermute(half(combine(total[k : k + 1], came)), ("z", "c"), Z_STEP)
-    plain = lambda v: v[0, :DATA].astype(F32) * fourth(scale_row(v)[0])
-    came = (plain(came) + jnp.where(c == 0, 0.0, plain(total[0:1]))).reshape(2, 2, 32, -1)
+        came = lax.ppermute(came, ("z", "c"), Z_STEP)
+        if k < 3:
+            came = half(combine(total[k + 1 : k + 2], came))
+    plain = lambda v: v[0, :DATA].astype(F32) * fourth(scale_rows(v)[0][0])
+    came = (plain(came) + jnp.where(c == 0, plain(straight), plain(total[0:1]))).reshape(2, 2, 32, -1)
     pick = lambda v, i, dim: lax.dynamic_index_in_dim(v, i, dim, keepdims=False)
     rows = pick(came, c, 1) + lax.ppermute(pick(came, 1 - c, 1), "c", SWAP)
     return (pick(rows, y, 0) + lax.ppermute(pick(rows, 1 - y, 0), "y", SWAP)) * factor
@@ -155,6 +188,7 @@
         ),
         out_shape=jax.ShapeDtypeStruct((rows, 4096), jnp.bfloat16),
         input_output_aliases={2 + count: 0} if extra else {},
+        compiler_params=pltpu.CompilerParams(vmem_limit_bytes=20 << 20),
         cost_estimate=pl.CostEstimate(flops=2 * rows * size * width, bytes_accessed=4 << 20, transcendentals=0),
     )(where, cot, *blocks, *extra)
 
@@ -179,7 +213,8 @@
     other = lax.ppermute(block, "c", SWAP)
     at = lambda k: (z + k * sign) % NZ
     grad = token_part((z, at(-1), at(1), 0, x), cot, [own, near[0], swapped[0]], None)
-    grad = token_part((at(-2), at(2), at(-3), at(3), x), cot, [near[1], swapped[1], near[2], swapped[2]], grad)
+    grad = token_part((at(-2), at(2), 0, 0, x), cot, [near[1], swapped[1]], grad)
+    grad = token_part((at(-3), at(3), 0, 0, x), cot, [near[2], swapped[2]], grad)
     return token_part((at(4), 0, 0, 0, x, 2 * c, 2 - 2 * c), cot, [block, other], grad, halves=True)
 
 

time: 161 us -> 144 us (0.89)
  other arithmetic: 20.5 us -> 9.62 us
  Pallas kernels: 32.2 us -> 26.1 us
  starting transfers between devices: 19.3 us -> 21.5 us
  waiting for transfers between devices: 78.8 us -> 76.7 us
    ppermute x3, waiting for transfers between devices: 19.6 us -> 30.9 us  [token_grads(): block = lax.ppermute(block, ('z', 'c'), Z_STEP)]
    ppermute x1, waiting for transfers between devices: 7.8 us -> 0.01 us  [sum_grad(): other_cot = lax.ppermute(cot, 'c', SWAP)]
    slice x1, other arithmetic: 5.13 us -> 1.02 us  [grad_terms(): terms[4 * BLOCK * k:4 * BLOCK * (k + 1)]]
    pallas_call x3 -> x4, Pallas kernels: 17.2 us -> 13.1 us  [token_part(): pl.pallas_call(functools.partial(token_kernel, count=count, halves=halves...]
    ppermute x1, waiting for transfers between devices: 3.22 us -> 0.01 us  [token_grads(): other = lax.ppermute(weight, 'y', SWAP)]
    convert_element_type x5 -> x4, other arithmetic: 5.47 us -> 2.97 us  [sum_grad(): half = lambda v: v.astype(jnp.float16)]
    ppermute x5 -> x6, starting transfers between devices: 4.17 us -> 6.56 us  [the longest x1 6.45 us: sum_grad(): straight = lax.ppermute(half(total[0:1]), ('z', 'c'), Z_FAR)]
    unnamed x22 -> x20, local copies, waits for them, and re-layouts: 2.07 us -> 4.43 us
  transfers between devices with their start and end apart: 26 -> 27, of which waited for: 12 -> 11; matrix products, arithmetic and copies ran while one was open for 14% -> 8% of each run, Pallas kernels for 17% -> 17%
where the time goes in v1:
time: 144 us; the launch traced here: 142 us
  waiting for transfers between devices  76.7 us (53%)
  Pallas kernels  26.1 us (18%)
  starting transfers between devices  21.5 us (15%)
  other arithmetic  9.62 us (7%)
  local copies, waits for them, and re-layouts  6.9 us (5%)
    ppermute x3, waiting for transfers between devices, token_grads(): block = lax.ppermute(block, ('z', 'c'), Z_STEP)  30.9 us
    ppermute x3, waiting for transfers between devices, sum_grad(): came = lax.ppermute(came, ('z', 'c'), Z_STEP)  17.5 us
    pallas_call x4, Pallas kernels, token_part(): pl.pallas_call(functools.partial(token_kernel, count=count, halves=halves...  13.1 us
    ppermute x1, waiting for transfers between devices, sum_grad(): cross = lax.ppermute(cross, ('x', 'c'), X_STEP)  10.1 us
    ppermute x3, waiting for transfers between devices, token_grads(): others = [lax.ppermute(pair, 'x', ring(NX - k)) for k in (1, 2, 3)]  9.02 us
    pallas_call x2, Pallas kernels, grad_terms(): call(jnp.concatenate(chunks).astype(jnp.int32), *[tokens] * 4, others, co...  8.84 us
    ppermute x1, waiting for transfers between devices, sum_grad(): straight = lax.ppermute(half(total[0:1]), ('z', 'c'), Z_FAR)  6.54 us
    ppermute x1, starting transfers between devices, sum_grad(): straight = lax.ppermute(half(total[0:1]), ('z', 'c'), Z_FAR)  6.45 us
  transfers between devices with their start and end apart: 27, of which 11 were waited for; matrix products, arithmetic and copies ran while one was open for 8% of the time, Pallas kernels for 17%

profile of v1, /device:TPU:16, one launch (start us, length us, event | category | flops | bytes accessed | tf_op | source)
XLA Modules:
  0.0 141.8 jit_solution(15012320667519069676)
XLA Ops:
  0.8 2.2 %copy-done = bf16[512,4096]{1,0:T(8,128)(2,1)S(1)} copy-done((bf16[512,4096]{1,0:T(8,128)(2,1)S(1)}, bf16[512,4096]{1,0:T(8,128)(2,1)}, u32[]{:S(2)}) %copy-start) | copy-done | bytes 4194328
  3.0 2.6 %shard_map.97 = bf16[3,512,512]{2,1,0:T(8,128)(2,1)} custom-call(s32[12]{0:T(128)S(1)} %pad_add_fusion.3._, bf16[512,4096]{1,0:T(8,128)(2,1)S(1)} %copy-done, bf16[512,4096]{1,0:T(8,128)(2,1)S(1)} %copy-done, bf16[512,4096]{1,0:T(8,128)(2,1)S(1)} %copy-done, bf16[512,4096]{1,0:T(8,128)(2,1)S(1)} %copy-done), custom_call_target="tpu_custom_call" | custom-call | flops 786432 | bytes 3145728 | tf_op jit(solution)/shard_map/pallas_call | solution.py:61
  6.1 1.5 %shard_map.99 = bf16[1,512,512]{2,1,0:T(8,128)(2,1)} custom-call(s32[4]{0:T(128)S(1)} %get-tuple-element.36._, bf16[512,4096]{1,0:T(8,128)(2,1)S(1)} %copy-done.1, bf16[512,4096]{1,0:T(8,128)(2,1)S(1)} %copy-done.1, bf16[512,4096]{1,0:T(8,128)(2,1)S(1)} %copy-done.1, bf16[512,4096]{1,0:T(8,128)(2,1)S(1)} %copy-done.1), custom_call_target="tpu_custom_call" | custom-call | flops 262144 | bytes 1048576 | tf_op jit(solution)/shard_map/pallas_call | solution.py:61
  7.7 1.3 collective-permute-start
  9.0 2.4 %collective-permute-done.17.refs_4_ = bf16[1,512,512]{2,1,0:T(8,128)(2,1)S(1)} collective-permute-done((bf16[1,512,512]{2,1,0:T(8,128)(2,1)}, bf16[1,512,512]{2,1,0:T(8,128)(2,1)S(1)}, u32[]{:S(2)}, u32[]{:S(2)}) %collective-permute-start.17) | collective-permute-done | bytes 524320 | tf_op jit(solution)/shard_map/ppermute | solution.py:126
  11.5 2.2 %copy-done.2 = bf16[512,4096]{1,0:T(8,128)(2,1)S(1)} copy-done((bf16[512,4096]{1,0:T(8,128)(2,1)S(1)}, bf16[512,4096]{1,0:T(8,128)(2,1)}, u32[]{:S(2)}) %copy-start.2) | copy-done | bytes 4194328
  13.7 2.2 %shard_map.100 = f32[544,1024]{1,0:T(8,128)S(1)} custom-call(s32[4]{0:T(128)S(1)} %get-tuple-element.39._, bf16[512,4096]{1,0:T(8,128)(2,1)S(1)} %copy-done.2, bf16[512,4096]{1,0:T(8,128)(2,1)S(1)} %copy-done.2, bf16[512,4096]{1,0:T(8,128)(2,1)S(1)} %copy-done.2, bf16[512,4096]{1,0:T(8,128)(2,1)S(1)} %copy-done.2, ...), custom_call_target="tpu_custom_call" | custom-call | flops 1073741824 | bytes 5242880 | tf_op jit(solution)/shard_map/pallas_call | solution.py:109
  16.1 1.6 %collective-permute-start.18 = (f16[4,136,1024]{2,1,0:T(8,128)(2,1)S(1)}, f16[4,136,1024]{2,1,0:T(8,128)(2,1)S(1)}, u32[]{:S(2)}, u32[]{:S(2)}) collective-permute-start(f16[4,136,1024]{2,1,0:T(8,128)(2,1)S(1)} %bitcast.74), channel_id=1, source_target_pairs={{0,4},{1,13},{4,8},{5,1},{8,12},{9,5},{12,0},{13,9},{2,6},{3,15},{... | collective-permute-start | bytes 3342344 | tf_op jit(solution)/shard_map/ppermute | solution.py:129
  17.7 1.6 %collective-permute-start.3 = (bf16[2,32,1024]{2,1,0:T(8,128)(2,1)S(1)}, bf16[2,32,1024]{2,1,0:T(8,128)(2,1)S(1)}, u32[]{:S(2)}, u32[]{:S(2)}) collective-permute-start(bf16[2,32,1024]{2,1,0:T(8,128)(2,1)S(1)} %maximum_select_fusion.2), channel_id=1, source_target_pairs={{0,4},{4,8},{8,12},{12,0},{1,5},{5,9},{9,13},{13,1},{2,6},{6,10},{... | collective-permute-start | bytes 393224 | tf_op jit(solution)/shard_map/ppermute | solution.py:202
  19.2 1.7 %collective-permute-start.1 = (bf16[2,32,1024]{2,1,0:T(8,128)(2,1)S(1)}, bf16[2,32,1024]{2,1,0:T(8,128)(2,1)S(1)}, u32[]{:S(2)}, u32[]{:S(2)}) collective-permute-start(bf16[2,32,1024]{2,1,0:T(8,128)(2,1)S(1)} %maximum_select_fusion.2), channel_id=1, source_target_pairs={{0,12},{4,0},{8,4},{12,8},{1,13},{5,1},{9,5},{13,9},{2,14},{6,2},{... | collective-permute-start | bytes 393224 | tf_op jit(solution)/shard_map/ppermute | solution.py:202
  21.0 1.5 %collective-permute-start.2 = (bf16[2,32,1024]{2,1,0:T(8,128)(2,1)S(1)}, bf16[2,32,1024]{2,1,0:T(8,128)(2,1)S(1)}, u32[]{:S(2)}, u32[]{:S(2)}) collective-permute-start(bf16[2,32,1024]{2,1,0:T(8,128)(2,1)S(1)} %maximum_select_fusion.2), channel_id=1, source_target_pairs={{0,8},{4,12},{8,0},{12,4},{1,9},{5,13},{9,1},{13,5},{2,10},{6,14},... | collective-permute-start | bytes 393224 | tf_op jit(solution)/shard_map/ppermute | solution.py:202
  22.5 6.7 %shard_map.98 = f32[1632,1024]{1,0:T(8,128)S(1)} custom-call(s32[12]{0:T(128)S(1)} %pad_add_fusion.2._, bf16[512,4096]{1,0:T(8,128)(2,1)S(1)} %copy-done.2, bf16[512,4096]{1,0:T(8,128)(2,1)S(1)} %copy-done.2, bf16[512,4096]{1,0:T(8,128)(2,1)S(1)} %copy-done.2, bf16[512,4096]{1,0:T(8,128)(2,1)S(1)} %copy-done.2, ...), custom_call_target="tpu_custom_call" | custom-call | flops 3221225472 | bytes 11534336 | tf_op jit(solution)/shard_map/pallas_call | solution.py:109
  29.2 1.0 fusion.34
  30.3 6.7 %collective-permute-done.3 = bf16[2,32,1024]{2,1,0:T(8,128)(2,1)S(1)} collective-permute-done((bf16[2,32,1024]{2,1,0:T(8,128)(2,1)S(1)}, bf16[2,32,1024]{2,1,0:T(8,128)(2,1)S(1)}, u32[]{:S(2)}, u32[]{:S(2)}) %collective-permute-start.3) | collective-permute-done | bytes 131104 | tf_op jit(solution)/shard_map/ppermute | solution.py:202
  37.1 2.3 %collective-permute-done.2 = bf16[2,32,1024]{2,1,0:T(8,128)(2,1)S(1)} collective-permute-done((bf16[2,32,1024]{2,1,0:T(8,128)(2,1)S(1)}, bf16[2,32,1024]{2,1,0:T(8,128)(2,1)S(1)}, u32[]{:S(2)}, u32[]{:S(2)}) %collective-permute-start.2) | collective-permute-done | bytes 131104 | tf_op jit(solution)/shard_map/ppermute | solution.py:202
  40.3 10.1 %collective-permute-done.15 = f16[4,136,1024]{2,1,0:T(8,128)(2,1)S(1)} collective-permute-done((f16[4,136,1024]{2,1,0:T(8,128)(2,1)S(1)}, f16[4,136,1024]{2,1,0:T(8,128)(2,1)S(1)}, u32[]{:S(2)}, u32[]{:S(2)}) %collective-permute-start.15) | collective-permute-done | bytes 1114144 | tf_op jit(solution)/shard_map/ppermute | solution.py:135
  50.7 2.0 %collective-permute-start.5 = (bf16[512,1024]{1,0:T(8,128)(2,1)S(1)}, bf16[512,1024]{1,0:T(8,128)(2,1)S(1)}, u32[]{:S(2)}, u32[]{:S(2)}) collective-permute-start(bf16[512,1024]{1,0:T(8,128)(2,1)S(1)} %bitcast.66), channel_id=1, source_target_pairs={{0,16},{1,113},{16,32},{17,1},{32,48},{33,17},{48,64},{49,33},{64,... | collective-permute-start | bytes 3145736 | tf_op jit(solution)/shard_map/ppermute | solution.py:209
  52.7 16.7 %collective-permute-done.5.refs_2_ = bf16[512,1024]{1,0:T(8,128)(2,1)S(1)} collective-permute-done((bf16[512,1024]{1,0:T(8,128)(2,1)S(1)}, bf16[512,1024]{1,0:T(8,128)(2,1)S(1)}, u32[]{:S(2)}, u32[]{:S(2)}) %collective-permute-start.5) | collective-permute-done | bytes 1048608 | tf_op jit(solution)/shard_map/ppermute | solution.py:209
  71.3 14.2 %collective-permute-done.6.refs_1_ = bf16[512,1024]{1,0:T(8,128)(2,1)} collective-permute-done((bf16[512,1024]{1,0:T(8,128)(2,1)S(1)}, bf16[512,1024]{1,0:T(8,128)(2,1)}, u32[]{:S(2)}, u32[]{:S(2)}) %collective-permute-start.6) | collective-permute-done | bytes 1048608 | tf_op jit(solution)/shard_map/ppermute | solution.py:209
  85.5 2.9 %collective-permute-done.20 = f16[1,136,1024]{2,1,0:T(8,128)(2,1)S(1)} collective-permute-done((f16[1,136,1024]{2,1,0:T(8,128)(2,1)S(1)}, f16[1,136,1024]{2,1,0:T(8,128)(2,1)S(1)}, u32[]{:S(2)}, u32[]{:S(2)}) %collective-permute-start.20) | collective-permute-done | bytes 278560 | tf_op jit(solution)/shard_map/ppermute | solution.py:142
  90.9 1.1 slice.161
  92.0 12.7 %collective-permute-done.21 = f16[1,136,1024]{2,1,0:T(8,128)(2,1)S(1)} collective-permute-done((f16[1,136,1024]{2,1,0:T(8,128)(2,1)}, f16[1,136,1024]{2,1,0:T(8,128)(2,1)S(1)}, u32[]{:S(2)}, u32[]{:S(2)}) %collective-permute-start.21) | collective-permute-done | bytes 278560 | tf_op jit(solution)/shard_map/ppermute | solution.py:142
  104.7 6.5 %collective-permute-start.23 = (f16[1,136,1024]{2,1,0:T(8,128)(2,1)}, f16[1,136,1024]{2,1,0:T(8,128)(2,1)S(1)}, u32[]{:S(2)}, u32[]{:S(2)}) collective-permute-start(f16[1,136,1024]{2,1,0:T(8,128)(2,1)} %get-tuple-element.31), channel_id=1, source_target_pairs={{0,64},{16,80},{32,96},{48,112},{64,0},{80,16},{96,32},{112,48},{2... | collective-permute-start | bytes 835592 | tf_op jit(solution)/shard_map/ppermute | solution.py:139
  112.1 1.2 fusion.5
  113.5 6.5 %collective-permute-done.23 = f16[1,136,1024]{2,1,0:T(8,128)(2,1)S(1)} collective-permute-done((f16[1,136,1024]{2,1,0:T(8,128)(2,1)}, f16[1,136,1024]{2,1,0:T(8,128)(2,1)S(1)}, u32[]{:S(2)}, u32[]{:S(2)}) %collective-permute-start.23) | collective-permute-done | bytes 278560 | tf_op jit(solution)/shard_map/ppermute | solution.py:139
  121.0 1.9 %collective-permute-done.22 = f16[1,136,1024]{2,1,0:T(8,128)(2,1)S(1)} collective-permute-done((f16[1,136,1024]{2,1,0:T(8,128)(2,1)S(1)}, f16[1,136,1024]{2,1,0:T(8,128)(2,1)S(1)}, u32[]{:S(2)}, u32[]{:S(2)}) %collective-permute-start.22) | collective-permute-done | bytes 278560 | tf_op jit(solution)/shard_map/ppermute | solution.py:142
  124.0 2.4 %multiply_subtract_fusion = (f32[131072]{0:T(1024)}, f32[131072]{0:T(1024)}) fusion(f32[131072]{0:T(1024)S(1)} %copy-done.7, f32[131072]{0:T(1024)} %bitcast.53, f32[131072]{0:T(1024)} %collective-permute-done.26, f32[131072]{0:T(1024)S(1)} %copy-done.8), kind=kLoop, calls=%fused_computation.17 | loop fusion | flops 1179648 | bytes 3145728 | tf_op jit(solution)/shard_map/sub | solution.py:229
  126.4 3.8 %shard_map.93.refs_3_ = bf16[512,4096]{1,0:T(8,128)(2,1)} custom-call(s32[5]{0:T(128)S(1)} %stack.122.where, bf16[512,1024]{1,0:T(8,128)(2,1)S(1)} %copy-done.3, bf16[512,1024]{1,0:T(8,128)(2,1)S(1)} %bitcast.67, bf16[512,1024]{1,0:T(8,128)(2,1)S(1)} %copy-done.5, bf16[512,1024]{1,0:T(8,128)(2,1)S(1)} %collective-permute-done.12.refs_3_), custom_call_target="tpu_custom_call" | custom-call | flops 1610612736 | bytes 4194304 | tf_op jit(solution)/shard_map/pallas_call | solution.py:179
  130.4 4.2 %shard_map.94.refs_3_ = bf16[512,4096]{1,0:T(8,128)(2,1)} custom-call(s32[5]{0:T(128)S(1)} %get-tuple-element.42.where, bf16[512,1024]{1,0:T(8,128)(2,1)S(1)} %copy-done.3, bf16[512,1024]{1,0:T(8,128)(2,1)} %collective-permute-done.6.refs_1_, bf16[512,1024]{1,0:T(8,128)(2,1)S(1)} %collective-permute-done.11.refs_2_, ...), custom_call_target="tpu_custom_call", output_to_operand_aliasing={{}: (4, {})} | custom-call | flops 1073741824 | bytes 4194304 | tf_op jit(solution)/shard_map/pallas_call | solution.py:179
  134.7 1.4 collective-permute-start.25
  136.1 3.0 %shard_map.95.refs_3_ = bf16[512,4096]{1,0:T(8,128)(2,1)} custom-call(s32[5]{0:T(128)S(1)} %get-tuple-element.43.where, bf16[512,1024]{1,0:T(8,128)(2,1)S(1)} %copy-done.3, bf16[512,1024]{1,0:T(8,128)(2,1)S(1)} %collective-permute-done.7.refs_1_, bf16[512,1024]{1,0:T(8,128)(2,1)S(1)} %collective-permute-done.10.refs_2_, ...), custom_call_target="tpu_custom_call", output_to_operand_aliasing={{}: (4, {})} | custom-call | flops 1073741824 | bytes 4194304 | tf_op jit(solution)/shard_map/pallas_call | solution.py:179
  139.1 2.1 %shard_map.96 = bf16[512,4096]{1,0:T(8,128)(2,1)} custom-call(s32[7]{0:T(128)S(1)} %stack.97.where, bf16[512,1024]{1,0:T(8,128)(2,1)S(1)} %copy-done.3, bf16[256,1024]{1,0:T(8,128)(2,1)S(1)} %collective-permute-done.8.refs_1_, bf16[256,1024]{1,0:T(8,128)(2,1)S(1)} %collective-permute-done.9.refs_2_, ...), custom_call_target="tpu_custom_call", output_to_operand_aliasing={{}: (4, {})} | custom-call | flops 536870912 | bytes 4194304 | tf_op jit(solution)/shard_map/pallas_call | solution.py:179
  (92 shorter events, 10.6 us)
Async XLA Ops:
  3.0 3.1 %copy-start.1 = (bf16[512,4096]{1,0:T(8,128)(2,1)S(1)}, bf16[512,4096]{1,0:T(8,128)(2,1)}, u32[]{:S(2)}) copy-start(bf16[512,4096]{1,0:T(8,128)(2,1)} %refs_3_.7) | copy-start | bytes 12582916
  5.6 16.9 %collective-permute-start.13 = (bf16[3,512,512]{2,1,0:T(8,128)(2,1)}, bf16[3,512,512]{2,1,0:T(8,128)(2,1)}, u32[]{:S(2)}, u32[]{:S(2)}) collective-permute-start(bf16[3,512,512]{2,1,0:T(8,128)(2,1)} %shard_map.97), channel_id=1, source_target_pairs={{0,1},{1,0},{2,3},{3,2},{4,5},{5,4},{6,7},{7,6},{8,9},{9,8},{10,11... | collective-permute-start | bytes 4718600 | tf_op jit(solution)/shard_map/ppermute | solution.py:127
  5.6 5.9 %collective-permute-start.14 = (bf16[512,1024]{1,0:T(8,128)(2,1)S(1)}, bf16[512,1024]{1,0:T(8,128)(2,1)S(1)}, u32[]{:S(2)}, u32[]{:S(2)}) collective-permute-start(bf16[512,1024]{1,0:T(8,128)(2,1)S(1)} %copy-done.3), channel_id=1, source_target_pairs={{0,1},{1,0},{2,3},{3,2},{4,5},{5,4},{6,7},{7,6},{8,9},{9,8},{10,11... | collective-permute-start | bytes 3145736 | tf_op jit(solution)/shard_map/ppermute | solution.py:116
  7.7 3.8 %collective-permute-start.17 = (bf16[1,512,512]{2,1,0:T(8,128)(2,1)}, bf16[1,512,512]{2,1,0:T(8,128)(2,1)S(1)}, u32[]{:S(2)}, u32[]{:S(2)}) collective-permute-start(bf16[1,512,512]{2,1,0:T(8,128)(2,1)} %shard_map.99), channel_id=1, source_target_pairs={{0,1},{1,0},{2,3},{3,2},{4,5},{5,4},{6,7},{7,6},{8,9},{9,8},{10,11... | collective-permute-start | bytes 1572872 | tf_op jit(solution)/shard_map/ppermute | solution.py:126
  7.7 10.0 %collective-permute-start = (bf16[32,1024]{1,0:T(8,128)(2,1)S(1)}, bf16[32,1024]{1,0:T(8,128)(2,1)S(1)}, u32[]{:S(2)}, u32[]{:S(2)}) collective-permute-start(bf16[32,1024]{1,0:T(8,128)(2,1)S(1)} %bitcast.78), channel_id=1, source_target_pairs={{0,2},{2,0},{1,3},{3,1},{4,6},{6,4},{5,7},{7,5},{8,10},{10,8},{9,1... | collective-permute-start | bytes 196616 | tf_op jit(solution)/shard_map/ppermute | solution.py:200
  16.1 23.5 %collective-permute-start.18 = (f16[4,136,1024]{2,1,0:T(8,128)(2,1)S(1)}, f16[4,136,1024]{2,1,0:T(8,128)(2,1)S(1)}, u32[]{:S(2)}, u32[]{:S(2)}) collective-permute-start(f16[4,136,1024]{2,1,0:T(8,128)(2,1)S(1)} %bitcast.74), channel_id=1, source_target_pairs={{0,4},{1,13},{4,8},{5,1},{8,12},{9,5},{12,0},{13,9},{2,6},{3,15},{... | collective-permute-start | bytes 3342344 | tf_op jit(solution)/shard_map/ppermute | solution.py:129
  17.7 19.4 %collective-permute-start.3 = (bf16[2,32,1024]{2,1,0:T(8,128)(2,1)S(1)}, bf16[2,32,1024]{2,1,0:T(8,128)(2,1)S(1)}, u32[]{:S(2)}, u32[]{:S(2)}) collective-permute-start(bf16[2,32,1024]{2,1,0:T(8,128)(2,1)S(1)} %maximum_select_fusion.2), channel_id=1, source_target_pairs={{0,4},{4,8},{8,12},{12,0},{1,5},{5,9},{9,13},{13,1},{2,6},{6,10},{... | collective-permute-start | bytes 393224 | tf_op jit(solution)/shard_map/ppermute | solution.py:202
  19.2 17.8 %collective-permute-start.1 = (bf16[2,32,1024]{2,1,0:T(8,128)(2,1)S(1)}, bf16[2,32,1024]{2,1,0:T(8,128)(2,1)S(1)}, u32[]{:S(2)}, u32[]{:S(2)}) collective-permute-start(bf16[2,32,1024]{2,1,0:T(8,128)(2,1)S(1)} %maximum_select_fusion.2), channel_id=1, source_target_pairs={{0,12},{4,0},{8,4},{12,8},{1,13},{5,1},{9,5},{13,9},{2,14},{6,2},{... | collective-permute-start | bytes 393224 | tf_op jit(solution)/shard_map/ppermute | solution.py:202
  21.0 18.4 %collective-permute-start.2 = (bf16[2,32,1024]{2,1,0:T(8,128)(2,1)S(1)}, bf16[2,32,1024]{2,1,0:T(8,128)(2,1)S(1)}, u32[]{:S(2)}, u32[]{:S(2)}) collective-permute-start(bf16[2,32,1024]{2,1,0:T(8,128)(2,1)S(1)} %maximum_select_fusion.2), channel_id=1, source_target_pairs={{0,8},{4,12},{8,0},{12,4},{1,9},{5,13},{9,1},{13,5},{2,10},{6,14},... | collective-permute-start | bytes 393224 | tf_op jit(solution)/shard_map/ppermute | solution.py:202
  30.2 20.2 %collective-permute-start.15 = (f16[4,136,1024]{2,1,0:T(8,128)(2,1)S(1)}, f16[4,136,1024]{2,1,0:T(8,128)(2,1)S(1)}, u32[]{:S(2)}, u32[]{:S(2)}) collective-permute-start(f16[4,136,1024]{2,1,0:T(8,128)(2,1)S(1)} %bitcast.73), channel_id=1, source_target_pairs={{0,4},{1,13},{4,8},{5,1},{8,12},{9,5},{12,0},{13,9},{2,6},{3,15},{... | collective-permute-start | bytes 3342344 | tf_op jit(solution)/shard_map/ppermute | solution.py:135
  39.5 10.9 %collective-permute-start.4 = (bf16[4,2,32,1024]{3,2,1,0:T(8,128)(2,1)S(1)}, bf16[4,2,32,1024]{3,2,1,0:T(8,128)(2,1)S(1)}, u32[]{:S(2)}, u32[]{:S(2)}) collective-permute-start(bf16[4,2,32,1024]{3,2,1,0:T(8,128)(2,1)S(1)} %get-tuple-element.33), channel_id=1, source_target_pairs={{0,1},{1,0},{2,3},{3,2},{4,5},{5,4},{6,7},{7,6},{8,9},{9,8},{10,11... | collective-permute-start | bytes 1572872 | tf_op jit(solution)/shard_map/ppermute | solution.py:204
  40.2 29.2 %collective-permute-start.19 = (f16[4,136,1024]{2,1,0:T(8,128)(2,1)S(1)}, f16[4,136,1024]{2,1,0:T(8,128)(2,1)S(1)}, u32[]{:S(2)}, u32[]{:S(2)}) collective-permute-start(f16[4,136,1024]{2,1,0:T(8,128)(2,1)S(1)} %select_convert_fusion), channel_id=1, source_target_pairs={{0,4},{1,13},{4,8},{5,1},{8,12},{9,5},{12,0},{13,9},{2,6},{3,15},{... | collective-permute-start | bytes 3342344 | tf_op jit(solution)/shard_map/ppermute | solution.py:137
  50.4 19.0 %collective-permute-start.16 = (f16[4,136,1024]{2,1,0:T(8,128)(2,1)S(1)}, f16[4,136,1024]{2,1,0:T(8,128)(2,1)S(1)}, u32[]{:S(2)}, u32[]{:S(2)}) collective-permute-start(f16[4,136,1024]{2,1,0:T(8,128)(2,1)S(1)} %collective-permute-done.15), channel_id=1, source_target_pairs={{0,1},{1,0},{2,3},{3,2},{4,5},{5,4},{6,7},{7,6},{8,9},{9,8},{10,11... | collective-permute-start | bytes 3342344 | tf_op jit(solution)/shard_map/ppermute | solution.py:136
  50.7 18.7 %collective-permute-start.5 = (bf16[512,1024]{1,0:T(8,128)(2,1)S(1)}, bf16[512,1024]{1,0:T(8,128)(2,1)S(1)}, u32[]{:S(2)}, u32[]{:S(2)}) collective-permute-start(bf16[512,1024]{1,0:T(8,128)(2,1)S(1)} %bitcast.66), channel_id=1, source_target_pairs={{0,16},{1,113},{16,32},{17,1},{32,48},{33,17},{48,64},{49,33},{64,... | collective-permute-start | bytes 3145736 | tf_op jit(solution)/shard_map/ppermute | solution.py:209
  69.4 16.1 %collective-permute-start.6 = (bf16[512,1024]{1,0:T(8,128)(2,1)S(1)}, bf16[512,1024]{1,0:T(8,128)(2,1)}, u32[]{:S(2)}, u32[]{:S(2)}) collective-permute-start(bf16[512,1024]{1,0:T(8,128)(2,1)S(1)} %collective-permute-done.5.refs_2_), channel_id=1, source_target_pairs={{0,16},{1,113},{16,32},{17,1},{32,48},{33,17},{48,64},{49,33},{64,... | collective-permute-start | bytes 3145736 | tf_op jit(solution)/shard_map/ppermute | solution.py:209
  70.4 18.0 %copy-start.6 = (f32[4,136,1024]{2,1,0:T(8,128)}, f32[4,136,1024]{2,1,0:T(8,128)S(1)}, u32[]{:S(2)}) copy-start(f32[4,136,1024]{2,1,0:T(8,128)S(1)} %get-tuple-element.13) | copy-start | bytes 6684676
  71.3 17.1 %collective-permute-start.20 = (f16[1,136,1024]{2,1,0:T(8,128)(2,1)S(1)}, f16[1,136,1024]{2,1,0:T(8,128)(2,1)S(1)}, u32[]{:S(2)}, u32[]{:S(2)}) collective-permute-start(f16[1,136,1024]{2,1,0:T(8,128)(2,1)S(1)} %get-tuple-element.30), channel_id=1, source_target_pairs={{0,16},{1,113},{16,32},{17,1},{32,48},{33,17},{48,64},{49,33},{64,... | collective-permute-start | bytes 835592 | tf_op jit(solution)/shard_map/ppermute | solution.py:142
  85.5 27.8 %collective-permute-start.7 = (bf16[512,1024]{1,0:T(8,128)(2,1)}, bf16[512,1024]{1,0:T(8,128)(2,1)S(1)}, u32[]{:S(2)}, u32[]{:S(2)}) collective-permute-start(bf16[512,1024]{1,0:T(8,128)(2,1)} %collective-permute-done.6.refs_1_), channel_id=1, source_target_pairs={{0,16},{1,113},{16,32},{17,1},{32,48},{33,17},{48,64},{49,33},{64,... | collective-permute-start | bytes 3145736 | tf_op jit(solution)/shard_map/ppermute | solution.py:209
  89.3 15.4 %collective-permute-start.21 = (f16[1,136,1024]{2,1,0:T(8,128)(2,1)}, f16[1,136,1024]{2,1,0:T(8,128)(2,1)S(1)}, u32[]{:S(2)}, u32[]{:S(2)}) collective-permute-start(f16[1,136,1024]{2,1,0:T(8,128)(2,1)} %fusion.2), channel_id=1, source_target_pairs={{0,16},{1,113},{16,32},{17,1},{32,48},{33,17},{48,64},{49,33},{64,... | collective-permute-start | bytes 835592 | tf_op jit(solution)/shard_map/ppermute | solution.py:142
  89.3 33.8 %collective-permute-start.26 = (f32[131072]{0:T(1024)}, f32[131072]{0:T(1024)}, u32[]{:S(2)}, u32[]{:S(2)}) collective-permute-start(f32[131072]{0:T(1024)} %bitcast.53), channel_id=1, source_target_pairs={{0,128},{128,0},{1,129},{129,1},{2,130},{130,2},{3,131},{131,3},{4... | collective-permute-start | bytes 1572872 | tf_op jit(solution)/shard_map/ppermute | solution.py:223
  89.9 36.5 %collective-permute-start.12 = (bf16[512,1024]{1,0:T(8,128)(2,1)}, bf16[512,1024]{1,0:T(8,128)(2,1)S(1)}, u32[]{:S(2)}, u32[]{:S(2)}) collective-permute-start(bf16[512,1024]{1,0:T(8,128)(2,1)} %copy-done.4), channel_id=1, source_target_pairs={{0,1},{1,0},{2,3},{3,2},{4,5},{5,4},{6,7},{7,6},{8,9},{9,8},{10,11... | collective-permute-start | bytes 3145736 | tf_op jit(solution)/shard_map/ppermute | solution.py:211
  90.8 39.6 %collective-permute-start.11 = (bf16[512,1024]{1,0:T(8,128)(2,1)}, bf16[512,1024]{1,0:T(8,128)(2,1)S(1)}, u32[]{:S(2)}, u32[]{:S(2)}) collective-permute-start(bf16[512,1024]{1,0:T(8,128)(2,1)} %collective-permute-done.6.refs_1_), channel_id=1, source_target_pairs={{0,1},{1,0},{2,3},{3,2},{4,5},{5,4},{6,7},{7,6},{8,9},{9,8},{10,11... | collective-permute-start | bytes 3145736 | tf_op jit(solution)/shard_map/ppermute | solution.py:211
  104.7 15.3 %collective-permute-start.23 = (f16[1,136,1024]{2,1,0:T(8,128)(2,1)}, f16[1,136,1024]{2,1,0:T(8,128)(2,1)S(1)}, u32[]{:S(2)}, u32[]{:S(2)}) collective-permute-start(f16[1,136,1024]{2,1,0:T(8,128)(2,1)} %get-tuple-element.31), channel_id=1, source_target_pairs={{0,64},{16,80},{32,96},{48,112},{64,0},{80,16},{96,32},{112,48},{2... | collective-permute-start | bytes 835592 | tf_op jit(solution)/shard_map/ppermute | solution.py:139
  113.3 10.7 %copy-start.7 = (f32[131072]{0:T(1024)S(1)}, f32[131072]{0:T(1024)}, u32[]{:S(2)}) copy-start(f32[131072]{0:T(1024)} %param.9) | copy-start | bytes 1572868
  113.3 10.7 %copy-start.8 = (f32[131072]{0:T(1024)S(1)}, f32[131072]{0:T(1024)}, u32[]{:S(2)}) copy-start(f32[131072]{0:T(1024)} %param.11) | copy-start | bytes 1572868
  113.3 9.6 %collective-permute-start.22 = (f16[1,136,1024]{2,1,0:T(8,128)(2,1)S(1)}, f16[1,136,1024]{2,1,0:T(8,128)(2,1)S(1)}, u32[]{:S(2)}, u32[]{:S(2)}) collective-permute-start(f16[1,136,1024]{2,1,0:T(8,128)(2,1)S(1)} %fusion.5), channel_id=1, source_target_pairs={{0,16},{1,113},{16,32},{17,1},{32,48},{33,17},{48,64},{49,33},{64,... | collective-permute-start | bytes 835592 | tf_op jit(solution)/shard_map/ppermute | solution.py:142
  120.0 10.4 %collective-permute-start.8 = (bf16[256,1024]{1,0:T(8,128)(2,1)S(1)}, bf16[256,1024]{1,0:T(8,128)(2,1)S(1)}, u32[]{:S(2)}, u32[]{:S(2)}) collective-permute-start(bf16[256,1024]{1,0:T(8,128)(2,1)S(1)} %constant_dynamic-slice_fusion), channel_id=1, source_target_pairs={{0,16},{1,113},{16,32},{17,1},{32,48},{33,17},{48,64},{49,33},{64,... | collective-permute-start | bytes 1572872 | tf_op jit(solution)/shard_map/ppermute | solution.py:212
  122.9 13.2 %collective-permute-start.10 = (bf16[512,1024]{1,0:T(8,128)(2,1)S(1)}, bf16[512,1024]{1,0:T(8,128)(2,1)S(1)}, u32[]{:S(2)}, u32[]{:S(2)}) collective-permute-start(bf16[512,1024]{1,0:T(8,128)(2,1)S(1)} %collective-permute-done.7.refs_1_), channel_id=1, source_target_pairs={{0,1},{1,0},{2,3},{3,2},{4,5},{5,4},{6,7},{7,6},{8,9},{9,8},{10,11... | collective-permute-start | bytes 3145736 | tf_op jit(solution)/shard_map/ppermute | solution.py:211
  123.1 3.3 %copy-start.5 = (bf16[512,1024]{1,0:T(8,128)(2,1)S(1)}, bf16[512,1024]{1,0:T(8,128)(2,1)}, u32[]{:S(2)}) copy-start(bf16[512,1024]{1,0:T(8,128)(2,1)} %copy-done.4) | copy-start | bytes 3145732
  123.2 11.5 %collective-permute-start.24 = (f32[2,32,1024]{2,1,0:T(8,128)S(1)}, f32[2,32,1024]{2,1,0:T(8,128)S(1)}, u32[]{:S(2)}, u32[]{:S(2)}) collective-permute-start(f32[2,32,1024]{2,1,0:T(8,128)S(1)} %dynamic-slice_bitcast_fusion), channel_id=1, source_target_pairs={{0,1},{1,0},{2,3},{3,2},{4,5},{5,4},{6,7},{7,6},{8,9},{9,8},{10,11... | collective-permute-start | bytes 786440 | tf_op jit(solution)/shard_map/ppermute | solution.py:148
  130.4 8.6 %collective-permute-start.9 = (bf16[256,1024]{1,0:T(8,128)(2,1)S(1)}, bf16[256,1024]{1,0:T(8,128)(2,1)S(1)}, u32[]{:S(2)}, u32[]{:S(2)}) collective-permute-start(bf16[256,1024]{1,0:T(8,128)(2,1)S(1)} %collective-permute-done.8.refs_1_), channel_id=1, source_target_pairs={{0,1},{1,0},{2,3},{3,2},{4,5},{5,4},{6,7},{7,6},{8,9},{9,8},{10,11... | collective-permute-start | bytes 1572872 | tf_op jit(solution)/shard_map/ppermute | solution.py:213
  134.7 6.4 %collective-permute-start.25 = (f32[32,1024]{1,0:T(8,128)S(1)}, f32[32,1024]{1,0:T(8,128)S(1)}, u32[]{:S(2)}, u32[]{:S(2)}) collective-permute-start(f32[32,1024]{1,0:T(8,128)S(1)} %dynamic-slice_bitcast_fusion.1), channel_id=1, source_target_pairs={{0,2},{2,0},{1,3},{3,1},{4,6},{6,4},{5,7},{7,5},{8,10},{10,8},{9,1... | collective-permute-start | bytes 393224 | tf_op jit(solution)/shard_map/ppermute | solution.py:149
  (5 other events, 9.5 us)

commit v2 on v1

--- a/solution.py
+++ b/solution.py
@@ -47,12 +47,23 @@
     return with_tails(body, up, down)
 
 
-def pick_kernel(_, *refs):
-    refs[-1][0] = jnp.concatenate([r[...] for r in refs[:4]], axis=1)
-
-
-def column_specs(rows):
-    return [pl.BlockSpec((rows, DATA), functools.partial(lambda k, i, ids: (0, ids[4 * i + k]), k)) for k in range(4)]
+def chunk_copies(ids, tokens, place, sems, group):
+    return [
+        pltpu.make_async_copy(
+            tokens.at[:, pl.ds(pl.multiple_of(ids[4 * group + k] * DATA, DATA), DATA)],
+            place.at[group, :, pl.ds(k * DATA, DATA)],
+            sems.at[4 * group + k],
+        )
+        for k in range(4)
+    ]
+
+
+def pick_kernel(ids, tokens, out, sems):
+    copies = [copy for group in range(out.shape[0]) for copy in chunk_copies(ids, tokens, out, sems, group)]
+    for copy in copies:
+        copy.start()
+    for copy in copies:
+        copy.wait()
 
 
 def pick_columns(chunks, tokens):
@@ -62,21 +73,35 @@
         pick_kernel,
         grid_spec=pltpu.PrefetchScalarGridSpec(
             num_scalar_prefetch=1,
-            grid=(count,),
-            in_specs=column_specs(rows),
-            out_specs=pl.BlockSpec((1, rows, 512), lambda i, ids: (i, 0, 0)),
+            grid=(1,),
+            in_specs=[pl.BlockSpec(memory_space=pltpu.HBM)],
+            out_specs=pl.BlockSpec((count, rows, 512), lambda i, ids: (0, 0, 0)),
+            scratch_shapes=[pltpu.SemaphoreType.DMA((4 * count,))],
         ),
         out_shape=jax.ShapeDtypeStruct((count, rows, 512), tokens.dtype),
         compiler_params=pltpu.CompilerParams(vmem_limit_bytes=16 << 20),
         cost_estimate=pl.CostEstimate(flops=rows * 512 * count, bytes_accessed=count << 20, transcendentals=0),
-    )(jnp.concatenate(chunks).astype(jnp.int32), *[tokens] * 4)
-
-
-def term_kernel(_, *refs):
-    *cols, theirs, cot_a, cot_b, out = refs
+    )(jnp.concatenate(chunks).astype(jnp.int32), tokens)
+
+
+def term_kernel(ids, tokens, theirs, cot_a, cot_b, out, cols, sems, *, count):
+    step = pl.program_id(0)
+
+    @pl.when(step == 0)
+    def _():
+        for group in range(count):
+            for copy in chunk_copies(ids, tokens, cols, sems, group):
+                copy.start()
+
+    for group in range(count):
+
+        @pl.when(step == group)
+        def _():
+            for copy in chunk_copies(ids, tokens, cols, sems, group):
+                copy.wait()
+
     dims = (((0,), (0,)), ((), ()))
-    mine = jnp.concatenate([r[...] for r in cols], axis=1)
-    total = lax.dot_general(mine, cot_a[...], dims, preferred_element_type=F32)
+    total = lax.dot_general(cols[step], cot_a[...], dims, preferred_element_type=F32)
     total += lax.dot_general(theirs[0], cot_b[...], dims, preferred_element_type=F32)
     top = jnp.full((TAIL, out.shape[-1]), jnp.maximum(jnp.max(jnp.abs(total)), 1e-30), F32)
     power = jnp.clip(jnp.ceil((jnp.log2(top) - 8.5) * 0.25), -14.0, 14.0)
@@ -93,12 +118,21 @@
     count = len(chunks)
     whole = pl.BlockSpec((rows, width), lambda i, ids: (0, 0))
     call = pl.pallas_call(
-        term_kernel,
+        functools.partial(term_kernel, count=count),
         grid_spec=pltpu.PrefetchScalarGridSpec(
             num_scalar_prefetch=1,
             grid=(count,),
-            in_specs=column_specs(rows) + [pl.BlockSpec((1, rows, 512), lambda i, ids: (i, 0, 0)), whole, whole],
+            in_specs=[
+                pl.BlockSpec(memory_space=pltpu.HBM),
+                pl.BlockSpec((1, rows, 512), lambda i, ids: (i, 0, 0)),
+                whole,
+                whole,
+            ],
             out_specs=pl.BlockSpec((4 * BLOCK, width), lambda i, ids: (i, 0)),
+            scratch_shapes=[
+                pltpu.VMEM((count, rows, 512), tokens.dtype),
+                pltpu.SemaphoreType.DMA((4 * count,)),
+            ],
         ),
         out_shape=jax.ShapeDtypeStruct((4 * BLOCK * count, width), F32),
         compiler_params=pltpu.CompilerParams(vmem_limit_bytes=28 << 20),
@@ -106,7 +140,7 @@
             flops=4 * rows * 512 * width * count, bytes_accessed=(2 + 3 * count) << 20, transcendentals=0
         ),
     )
-    terms = call(jnp.concatenate(chunks).astype(jnp.int32), *[tokens] * 4, others, cot, other_cot)
+    terms = call(jnp.concatenate(chunks).astype(jnp.int32), tokens, others, cot, other_cot)
     return [tall(terms[4 * BLOCK * k : 4 * BLOCK * (k + 1)]) for k in range(count)]
 
 
@@ -135,15 +169,19 @@
     cross = lax.ppermute(cross, ("x", "c"), X_STEP)
     cross = lax.ppermute(cross, "c", SWAP)
     direct = lax.ppermute(half(combine(near_term, from_far)), ("x", "c"), X_STEP)
-    total = combine(own_term, cross, direct)
-    straight = lax.ppermute(half(total[0:1]), ("z", "c"), Z_FAR)
-    came = half(total[1:2])
+    held = lambda k: [v[k : k + 1] for v in (own_term, cross, direct)]
+    came = half(combine(*held(1)))
+    first = came
     for k in range(1, 4):
         came = lax.ppermute(came, ("z", "c"), Z_STEP)
         if k < 3:
-            came = half(combine(total[k + 1 : k + 2], came))
-    plain = lambda v: v[0, :DATA].astype(F32) * fourth(scale_rows(v)[0][0])
-    came = (plain(came) + jnp.where(c == 0, plain(straight), plain(total[0:1]))).reshape(2, 2, 32, -1)
+            came = half(combine(*held(k + 1), came))
+    rest, _ = lax.optimization_barrier((held(0), first))
+    last = combine(*rest)
+    straight = lax.ppermute(half(last), ("z", "c"), Z_FAR)
+    value = lambda v: v.astype(F32) * fourth(scale_rows(v)[0])
+    came = value(came) + jnp.where(c == 0, value(straight), value(last))
+    came = came[0, :DATA].reshape(2, 2, 32, -1)
     pick = lambda v, i, dim: lax.dynamic_index_in_dim(v, i, dim, keepdims=False)
     rows = pick(came, c, 1) + lax.ppermute(pick(came, 1 - c, 1), "c", SWAP)
     return (pick(rows, y, 0) + lax.ppermute(pick(rows, 1 - y, 0), "y", SWAP)) * factor

time: 144 us -> 139 us (0.965)
  waiting for transfers between devices: 76.7 us -> 58 us
  other arithmetic: 9.62 us -> 15.5 us
  local copies, waits for them, and re-layouts: 6.9 us -> 11 us
  starting transfers between devices: 21.5 us -> 25.5 us
    ppermute x3, waiting for transfers between devices: 30.9 us -> 12.5 us  [token_grads(): block = lax.ppermute(block, ('z', 'c'), Z_STEP)]
    ppermute x3, waiting for transfers between devices: 9.02 us -> 0.01 us  [token_grads(): others = [lax.ppermute(pair, 'x', ring(NX - k)) for k in (1, 2, 3)]]
    ppermute x3, waiting for transfers between devices: 17.5 us -> 23.4 us  [sum_grad(): came = lax.ppermute(came, ('z', 'c'), Z_STEP)]
    mul x10 -> x13, other arithmetic: 0.98 us -> 4.82 us  [fourth(): return v * v * (v * v)]
    convert_element_type x4 -> x6, other arithmetic: 2.97 us -> 6.5 us  [sum_grad(): half = lambda v: v.astype(jnp.float16)]
    ppermute x1, waiting for transfers between devices: 0.01 us -> 3.04 us  [token_grads(): other = lax.ppermute(weight, 'y', SWAP)]
    ppermute x3, starting transfers between devices: 1.01 us -> 3.95 us  [token_grads(): swapped.append(lax.ppermute(block, 'c', SWAP))]
    ppermute x1, waiting for transfers between devices: 0.01 us -> 2.71 us  [sum_grad(): from_far = lax.ppermute(half(far_term), ('x', 'c'), X_STEP)]
  transfers between devices with their start and end apart: 27 -> 27, of which waited for: 11 -> 10; matrix products, arithmetic and copies ran while one was open for 8% -> 14% of each run, Pallas kernels for 17% -> 17%
where the time goes in v2:
time: 139 us; the launch traced here: 136 us
  waiting for transfers between devices  58 us (42%)
  starting transfers between devices  25.5 us (18%)
  Pallas kernels  25.2 us (18%)
  other arithmetic  15.5 us (11%)
  local copies, waits for them, and re-layouts  11 us (8%)
    ppermute x3, waiting for transfers between devices, sum_grad(): came = lax.ppermute(came, ('z', 'c'), Z_STEP)  23.4 us
    pallas_call x4, Pallas kernels, token_part(): pl.pallas_call(functools.partial(token_kernel, count=count, halves=halves...  13.1 us
    ppermute x3, waiting for transfers between devices, token_grads(): block = lax.ppermute(block, ('z', 'c'), Z_STEP)  12.5 us
    ppermute x1, waiting for transfers between devices, sum_grad(): cross = lax.ppermute(cross, ('x', 'c'), X_STEP)  10.4 us
    pallas_call x2, Pallas kernels, grad_terms(): call(jnp.concatenate(chunks).astype(jnp.int32), tokens, others, cot, othe...  9.17 us
    unnamed x16, local copies, waits for them, and re-layouts  6.88 us
    convert_element_type x6, other arithmetic, sum_grad(): half = lambda v: v.astype(jnp.float16)  6.5 us
    ppermute x1, starting transfers between devices, sum_grad(): straight = lax.ppermute(half(last), ('z', 'c'), Z_FAR)  6.46 us
  transfers between devices with their start and end apart: 27, of which 10 were waited for; matrix products, arithmetic and copies ran while one was open for 14% of the time, Pallas kernels for 17%

profile of v2, /device:TPU:16, one launch (start us, length us, event | category | flops | bytes accessed | tf_op | source)
XLA Modules:
  0.0 136.4 jit_solution(15503418052202147115)
XLA Ops:
  0.9 2.2 %copy-done = bf16[512,4096]{1,0:T(8,128)(2,1)S(1)} copy-done((bf16[512,4096]{1,0:T(8,128)(2,1)S(1)}, bf16[512,4096]{1,0:T(8,128)(2,1)}, u32[]{:S(2)}) %copy-start) | copy-done | bytes 4194328
  3.0 2.3 %shard_map.97 = bf16[3,512,512]{2,1,0:T(8,128)(2,1)} custom-call(s32[12]{0:T(128)S(1)} %pad_add_fusion.3.ids, bf16[512,4096]{1,0:T(8,128)(2,1)S(1)} %copy-done), custom_call_target="tpu_custom_call" | custom-call | flops 786432 | bytes 3145728 | tf_op jit(solution)/shard_map/pallas_call | solution.py:72
  8.4 3.0 %collective-permute-done = bf16[32,1024]{1,0:T(8,128)(2,1)S(1)} collective-permute-done((bf16[32,1024]{1,0:T(8,128)(2,1)S(1)}, bf16[32,1024]{1,0:T(8,128)(2,1)S(1)}, u32[]{:S(2)}, u32[]{:S(2)}) %collective-permute-start) | collective-permute-done | bytes 65568 | tf_op jit(solution)/shard_map/ppermute | solution.py:238
  11.5 1.6 %collective-permute-start.3 = (bf16[2,32,1024]{2,1,0:T(8,128)(2,1)S(1)}, bf16[2,32,1024]{2,1,0:T(8,128)(2,1)S(1)}, u32[]{:S(2)}, u32[]{:S(2)}) collective-permute-start(bf16[2,32,1024]{2,1,0:T(8,128)(2,1)S(1)} %maximum_select_fusion.2), channel_id=1, source_target_pairs={{0,4},{4,8},{8,12},{12,0},{1,5},{5,9},{9,13},{13,1},{2,6},{6,10},{... | collective-permute-start | bytes 393224 | tf_op jit(solution)/shard_map/ppermute | solution.py:240
  13.1 1.7 %collective-permute-start.1 = (bf16[2,32,1024]{2,1,0:T(8,128)(2,1)S(1)}, bf16[2,32,1024]{2,1,0:T(8,128)(2,1)S(1)}, u32[]{:S(2)}, u32[]{:S(2)}) collective-permute-start(bf16[2,32,1024]{2,1,0:T(8,128)(2,1)S(1)} %maximum_select_fusion.2), channel_id=1, source_target_pairs={{0,12},{4,0},{8,4},{12,8},{1,13},{5,1},{9,5},{13,9},{2,14},{6,2},{... | collective-permute-start | bytes 393224 | tf_op jit(solution)/shard_map/ppermute | solution.py:240
  14.8 1.8 %collective-permute-start.2 = (bf16[2,32,1024]{2,1,0:T(8,128)(2,1)S(1)}, bf16[2,32,1024]{2,1,0:T(8,128)(2,1)S(1)}, u32[]{:S(2)}, u32[]{:S(2)}) collective-permute-start(bf16[2,32,1024]{2,1,0:T(8,128)(2,1)S(1)} %maximum_select_fusion.2), channel_id=1, source_target_pairs={{0,8},{4,12},{8,0},{12,4},{1,9},{5,13},{9,1},{13,5},{2,10},{6,14},... | collective-permute-start | bytes 393224 | tf_op jit(solution)/shard_map/ppermute | solution.py:240
  16.7 2.2 %copy-done.2 = bf16[512,4096]{1,0:T(8,128)(2,1)S(1)} copy-done((bf16[512,4096]{1,0:T(8,128)(2,1)S(1)}, bf16[512,4096]{1,0:T(8,128)(2,1)}, u32[]{:S(2)}) %copy-start.2) | copy-done | bytes 4194328
  18.8 2.3 %shard_map.100 = f32[544,1024]{1,0:T(8,128)S(1)} custom-call(s32[4]{0:T(128)S(1)} %get-tuple-element.28.ids, bf16[512,4096]{1,0:T(8,128)(2,1)S(1)} %copy-done.2, bf16[1,512,512]{2,1,0:T(8,128)(2,1)S(1)} %collective-permute-done.17.theirs, bf16[512,1024]{1,0:T(8,128)(2,1)S(1)} %copy-done.3, bf16[512,1024]{1,0:T(8,128)(2,1)S(1)} %collective-permute-done.14.cot_b), custom_call_target="tpu_custom_call" | custom-call | flops 1073741824 | bytes 5242880 | tf_op jit(solution)/shard_map/pallas_call | solution.py:143
  22.2 6.9 %shard_map.98 = f32[1632,1024]{1,0:T(8,128)S(1)} custom-call(s32[12]{0:T(128)S(1)} %pad_add_fusion.2.ids, bf16[512,4096]{1,0:T(8,128)(2,1)S(1)} %copy-done.2, bf16[3,512,512]{2,1,0:T(8,128)(2,1)} %collective-permute-done.13.theirs, bf16[512,1024]{1,0:T(8,128)(2,1)S(1)} %copy-done.3, bf16[512,1024]{1,0:T(8,128)(2,1)S(1)} %collective-permute-done.14.cot_b), custom_call_target="tpu_custom_call" | custom-call | flops 3221225472 | bytes 11534336 | tf_op jit(solution)/shard_map/pallas_call | solution.py:143
  29.6 2.3 %copy-done.4 = f32[1632,1024]{1,0:T(8,128)} copy-done((f32[1632,1024]{1,0:T(8,128)}, f32[1632,1024]{1,0:T(8,128)S(1)}, u32[]{:S(2)}) %copy-start.4) | copy-done | bytes 6684696
  33.2 2.2 %collective-permute-start.5 = (bf16[512,1024]{1,0:T(8,128)(2,1)S(1)}, bf16[512,1024]{1,0:T(8,128)(2,1)S(1)}, u32[]{:S(2)}, u32[]{:S(2)}) collective-permute-start(bf16[512,1024]{1,0:T(8,128)(2,1)S(1)} %bitcast.106), channel_id=1, source_target_pairs={{0,16},{1,113},{16,32},{17,1},{32,48},{33,17},{48,64},{49,33},{64,... | collective-permute-start | bytes 3145736 | tf_op jit(solution)/shard_map/ppermute | solution.py:247
  35.4 2.7 %collective-permute-done.18 = f16[4,136,1024]{2,1,0:T(8,128)(2,1)S(1)} collective-permute-done((f16[4,136,1024]{2,1,0:T(8,128)(2,1)S(1)}, f16[4,136,1024]{2,1,0:T(8,128)(2,1)S(1)}, u32[]{:S(2)}, u32[]{:S(2)}) %collective-permute-start.18) | collective-permute-done | bytes 1114144 | tf_op jit(solution)/shard_map/ppermute | solution.py:163
  38.2 1.6 %select_convert_fusion = f16[4,136,1024]{2,1,0:T(8,128)(2,1)} fusion(f16[4,136,1024]{2,1,0:T(8,128)(2,1)S(1)} %collective-permute-done.18, f32[4,136,1024]{2,1,0:T(8,128)S(1)} %bitcast.109, f32[1024]{0:T(1024)S(1)} %bitcast.124, f32[1024]{0:T(1024)S(1)} %bitcast.140, f32[1024]{0:T(1024)S(1)} %bitcast.141, f32[1024]{0:T(1024)S(1)} %bitcast.139, ...), kind=kLoop, calls=%fused_computation.1 | loop fusion | flops 3899392 | bytes 4473104 | tf_op jit(solution)/shard_map/convert_element_type | solution.py:151
  39.7 10.4 %collective-permute-done.15 = f16[4,136,1024]{2,1,0:T(8,128)(2,1)} collective-permute-done((f16[4,136,1024]{2,1,0:T(8,128)(2,1)S(1)}, f16[4,136,1024]{2,1,0:T(8,128)(2,1)}, u32[]{:S(2)}, u32[]{:S(2)}) %collective-permute-start.15) | collective-permute-done | bytes 1114144 | tf_op jit(solution)/shard_map/ppermute | solution.py:169
  50.2 1.9 %collective-permute-done.5.refs_2_ = bf16[512,1024]{1,0:T(8,128)(2,1)S(1)} collective-permute-done((bf16[512,1024]{1,0:T(8,128)(2,1)S(1)}, bf16[512,1024]{1,0:T(8,128)(2,1)S(1)}, u32[]{:S(2)}, u32[]{:S(2)}) %collective-permute-start.5) | collective-permute-done | bytes 1048608 | tf_op jit(solution)/shard_map/ppermute | solution.py:247
  52.7 1.7 %slice_bitcast_fusion.3 = (f32[1,136,1024]{2,1,0:T(8,128)S(1)}, f32[1,136,1024]{2,1,0:T(8,128)S(1)}, f32[1,136,1024]{2,1,0:T(8,128)S(1)}, f32[1,136,1024]{2,1,0:T(8,128)S(1)}) fusion(f32[1632,1024]{1,0:T(8,128)} %copy-done.4), kind=kLoop, calls=%fused_computation.28 | loop fusion | bytes 4456448 | tf_op jit(solution)/shard_map/slice | solution.py:172
  54.4 3.9 %collective-permute-start.12 = (bf16[512,1024]{1,0:T(8,128)(2,1)S(1)}, bf16[512,1024]{1,0:T(8,128)(2,1)S(1)}, u32[]{:S(2)}, u32[]{:S(2)}) collective-permute-start(bf16[512,1024]{1,0:T(8,128)(2,1)S(1)} %collective-permute-done.5.refs_2_), channel_id=1, source_target_pairs={{0,1},{1,0},{2,3},{3,2},{4,5},{5,4},{6,7},{7,6},{8,9},{9,8},{10,11... | collective-permute-start | bytes 3145736 | tf_op jit(solution)/shard_map/ppermute | solution.py:249
  58.4 10.5 %collective-permute-done.6.refs_1_ = bf16[512,1024]{1,0:T(8,128)(2,1)} collective-permute-done((bf16[512,1024]{1,0:T(8,128)(2,1)S(1)}, bf16[512,1024]{1,0:T(8,128)(2,1)}, u32[]{:S(2)}, u32[]{:S(2)}) %collective-permute-start.6) | collective-permute-done | bytes 1048608 | tf_op jit(solution)/shard_map/ppermute | solution.py:247
  71.5 1.4 %fusion.10 = f16[1,136,1024]{2,1,0:T(8,128)(2,1)S(1)} fusion(f32[1632,1024]{1,0:T(8,128)} %copy-done.4, f16[4,136,1024]{2,1,0:T(8,128)(2,1)} %collective-permute-done.19, f16[4,136,1024]{2,1,0:T(8,128)(2,1)} %collective-permute-done.16, f32[1024]{0:T(1024)S(1)} %bitcast.123, f32[1024]{0:T(1024)S(1)} %bitcast.135, f32[1024]{0:T(1024)S(1)} %bitcast.143, ...), kind=kLoop, calls=%fused_computation.17 | loop fusion | flops 1392640 | bytes 1413392 | tf_op jit(solution)/shard_map/convert_element_type | solution.py:151
  74.1 14.0 %collective-permute-done.20 = f16[1,136,1024]{2,1,0:T(8,128)(2,1)S(1)} collective-permute-done((f16[1,136,1024]{2,1,0:T(8,128)(2,1)S(1)}, f16[1,136,1024]{2,1,0:T(8,128)(2,1)S(1)}, u32[]{:S(2)}, u32[]{:S(2)}) %collective-permute-start.20) | collective-permute-done | bytes 278560 | tf_op jit(solution)/shard_map/ppermute | solution.py:176
  89.7 1.5 %fusion.7 = f16[1,136,1024]{2,1,0:T(8,128)(2,1)S(1)} fusion(f16[1,136,1024]{2,1,0:T(8,128)(2,1)S(1)} %collective-permute-done.20, f32[1632,1024]{1,0:T(8,128)} %copy-done.4, f16[4,136,1024]{2,1,0:T(8,128)(2,1)} %collective-permute-done.19, f16[4,136,1024]{2,1,0:T(8,128)(2,1)} %collective-permute-done.16, f32[1024]{0:T(1024)S(1)} %bitcast.126, ...), kind=kLoop, calls=%fused_computation.13 | loop fusion | flops 1810432 | bytes 1696016 | tf_op jit(solution)/shard_map/convert_element_type | solution.py:151
  91.6 7.5 %collective-permute-done.21 = f16[1,136,1024]{2,1,0:T(8,128)(2,1)S(1)} collective-permute-done((f16[1,136,1024]{2,1,0:T(8,128)(2,1)S(1)}, f16[1,136,1024]{2,1,0:T(8,128)(2,1)S(1)}, u32[]{:S(2)}, u32[]{:S(2)}) %collective-permute-start.21) | collective-permute-done | bytes 278560 | tf_op jit(solution)/shard_map/ppermute | solution.py:176
  99.1 6.5 %collective-permute-start.23 = (f16[1,136,1024]{2,1,0:T(8,128)(2,1)S(1)}, f16[1,136,1024]{2,1,0:T(8,128)(2,1)S(1)}, u32[]{:S(2)}, u32[]{:S(2)}) collective-permute-start(f16[1,136,1024]{2,1,0:T(8,128)(2,1)S(1)} %get-tuple-element.14), channel_id=1, source_target_pairs={{0,64},{16,80},{32,96},{48,112},{64,0},{80,16},{96,32},{112,48},{2... | collective-permute-start | bytes 835592 | tf_op jit(solution)/shard_map/ppermute | solution.py:181
  107.1 1.5 %fusion.3 = f16[1,136,1024]{2,1,0:T(8,128)(2,1)S(1)} fusion(f16[1,136,1024]{2,1,0:T(8,128)(2,1)S(1)} %collective-permute-done.21, f32[1632,1024]{1,0:T(8,128)} %copy-done.4, f16[4,136,1024]{2,1,0:T(8,128)(2,1)} %collective-permute-done.19, f16[4,136,1024]{2,1,0:T(8,128)(2,1)} %collective-permute-done.16, f32[1024]{0:T(1024)S(1)} %bitcast.125, ...), kind=kLoop, calls=%fused_computation.8 | loop fusion | flops 1810432 | bytes 1696016 | tf_op jit(solution)/shard_map/convert_element_type | solution.py:151
  108.8 5.3 %collective-permute-done.23 = f16[1,136,1024]{2,1,0:T(8,128)(2,1)S(1)} collective-permute-done((f16[1,136,1024]{2,1,0:T(8,128)(2,1)S(1)}, f16[1,136,1024]{2,1,0:T(8,128)(2,1)S(1)}, u32[]{:S(2)}, u32[]{:S(2)}) %collective-permute-start.23) | collective-permute-done | bytes 278560 | tf_op jit(solution)/shard_map/ppermute | solution.py:181
  115.1 1.9 %collective-permute-done.22 = f16[1,136,1024]{2,1,0:T(8,128)(2,1)S(1)} collective-permute-done((f16[1,136,1024]{2,1,0:T(8,128)(2,1)S(1)}, f16[1,136,1024]{2,1,0:T(8,128)(2,1)S(1)}, u32[]{:S(2)}, u32[]{:S(2)}) %collective-permute-start.22) | collective-permute-done | bytes 278560 | tf_op jit(solution)/shard_map/ppermute | solution.py:176
  118.1 2.3 %multiply_subtract_fusion = (f32[131072]{0:T(1024)}, f32[131072]{0:T(1024)}) fusion(f32[131072]{0:T(1024)S(1)} %copy-done.5, f32[131072]{0:T(1024)} %bitcast.66, f32[131072]{0:T(1024)} %collective-permute-done.26, f32[131072]{0:T(1024)S(1)} %copy-done.6), kind=kLoop, calls=%fused_computation.23 | loop fusion | flops 1179648 | bytes 3145728 | tf_op jit(solution)/shard_map/sub | solution.py:267
  120.4 3.8 %shard_map.93.refs_3_ = bf16[512,4096]{1,0:T(8,128)(2,1)} custom-call(s32[5]{0:T(128)S(1)} %stack.122.where, bf16[512,1024]{1,0:T(8,128)(2,1)S(1)} %copy-done.3, bf16[512,1024]{1,0:T(8,128)(2,1)S(1)} %bitcast.107, bf16[512,1024]{1,0:T(8,128)(2,1)S(1)} %collective-permute-done.5.refs_2_, bf16[512,1024]{1,0:T(8,128)(2,1)S(1)} %collective-permute-done.12.refs_3_), custom_call_target="tpu_custom_call" | custom-call | flops 1610612736 | bytes 4194304 | tf_op jit(solution)/shard_map/pallas_call | solution.py:217
  124.8 4.2 %shard_map.94.refs_3_ = bf16[512,4096]{1,0:T(8,128)(2,1)} custom-call(s32[5]{0:T(128)S(1)} %get-tuple-element.59.where, bf16[512,1024]{1,0:T(8,128)(2,1)S(1)} %copy-done.3, bf16[512,1024]{1,0:T(8,128)(2,1)} %collective-permute-done.6.refs_1_, bf16[512,1024]{1,0:T(8,128)(2,1)S(1)} %collective-permute-done.11.refs_2_, ...), custom_call_target="tpu_custom_call", output_to_operand_aliasing={{}: (4, {})} | custom-call | flops 1073741824 | bytes 4194304 | tf_op jit(solution)/shard_map/pallas_call | solution.py:217
  129.1 1.5 %collective-permute-start.25 = (f32[32,1024]{1,0:T(8,128)S(1)}, f32[32,1024]{1,0:T(8,128)S(1)}, u32[]{:S(2)}, u32[]{:S(2)}) collective-permute-start(f32[32,1024]{1,0:T(8,128)S(1)} %dynamic-slice_bitcast_fusion.1), channel_id=1, source_target_pairs={{0,2},{2,0},{1,3},{3,1},{4,6},{6,4},{5,7},{7,5},{8,10},{10,8},{9,1... | collective-permute-start | bytes 393224 | tf_op jit(solution)/shard_map/ppermute | solution.py:187
  130.6 3.0 %shard_map.95.refs_3_ = bf16[512,4096]{1,0:T(8,128)(2,1)} custom-call(s32[5]{0:T(128)S(1)} %get-tuple-element.60.where, bf16[512,1024]{1,0:T(8,128)(2,1)S(1)} %copy-done.3, bf16[512,1024]{1,0:T(8,128)(2,1)S(1)} %collective-permute-done.7.refs_1_, bf16[512,1024]{1,0:T(8,128)(2,1)S(1)} %collective-permute-done.10.refs_2_, ...), custom_call_target="tpu_custom_call", output_to_operand_aliasing={{}: (4, {})} | custom-call | flops 1073741824 | bytes 4194304 | tf_op jit(solution)/shard_map/pallas_call | solution.py:217
  133.6 2.1 %shard_map.96 = bf16[512,4096]{1,0:T(8,128)(2,1)} custom-call(s32[7]{0:T(128)S(1)} %stack.97.where, bf16[512,1024]{1,0:T(8,128)(2,1)S(1)} %copy-done.3, bf16[256,1024]{1,0:T(8,128)(2,1)S(1)} %collective-permute-done.8.refs_1_, bf16[256,1024]{1,0:T(8,128)(2,1)S(1)} %collective-permute-done.9.refs_2_, ...), custom_call_target="tpu_custom_call", output_to_operand_aliasing={{}: (4, {})} | custom-call | flops 536870912 | bytes 4194304 | tf_op jit(solution)/shard_map/pallas_call | solution.py:217
  (92 shorter events, 17.4 us)
Async XLA Ops:
  3.0 2.4 %copy-start.3 = (bf16[512,1024]{1,0:T(8,128)(2,1)S(1)}, bf16[512,1024]{1,0:T(8,128)(2,1)}, u32[]{:S(2)}) copy-start(bf16[512,1024]{1,0:T(8,128)(2,1)} %cot_a.3) | copy-start | bytes 3145732
  3.0 3.1 %copy-start.1 = (bf16[512,4096]{1,0:T(8,128)(2,1)S(1)}, bf16[512,4096]{1,0:T(8,128)(2,1)}, u32[]{:S(2)}) copy-start(bf16[512,4096]{1,0:T(8,128)(2,1)} %tokens.7) | copy-start | bytes 12582916
  5.3 16.9 %collective-permute-start.13 = (bf16[3,512,512]{2,1,0:T(8,128)(2,1)}, bf16[3,512,512]{2,1,0:T(8,128)(2,1)}, u32[]{:S(2)}, u32[]{:S(2)}) collective-permute-start(bf16[3,512,512]{2,1,0:T(8,128)(2,1)} %shard_map.97), channel_id=1, source_target_pairs={{0,1},{1,0},{2,3},{3,2},{4,5},{5,4},{6,7},{7,6},{8,9},{9,8},{10,11... | collective-permute-start | bytes 4718600 | tf_op jit(solution)/shard_map/ppermute | solution.py:161
  5.4 11.2 %collective-permute-start.14 = (bf16[512,1024]{1,0:T(8,128)(2,1)S(1)}, bf16[512,1024]{1,0:T(8,128)(2,1)S(1)}, u32[]{:S(2)}, u32[]{:S(2)}) collective-permute-start(bf16[512,1024]{1,0:T(8,128)(2,1)S(1)} %copy-done.3), channel_id=1, source_target_pairs={{0,1},{1,0},{2,3},{3,2},{4,5},{5,4},{6,7},{7,6},{8,9},{9,8},{10,11... | collective-permute-start | bytes 3145736 | tf_op jit(solution)/shard_map/ppermute | solution.py:150
  6.9 7.9 %collective-permute-start.17 = (bf16[1,512,512]{2,1,0:T(8,128)(2,1)S(1)}, bf16[1,512,512]{2,1,0:T(8,128)(2,1)S(1)}, u32[]{:S(2)}, u32[]{:S(2)}) collective-permute-start(bf16[1,512,512]{2,1,0:T(8,128)(2,1)S(1)} %shard_map.99), channel_id=1, source_target_pairs={{0,1},{1,0},{2,3},{3,2},{4,5},{5,4},{6,7},{7,6},{8,9},{9,8},{10,11... | collective-permute-start | bytes 1572872 | tf_op jit(solution)/shard_map/ppermute | solution.py:160
  7.0 4.5 %collective-permute-start = (bf16[32,1024]{1,0:T(8,128)(2,1)S(1)}, bf16[32,1024]{1,0:T(8,128)(2,1)S(1)}, u32[]{:S(2)}, u32[]{:S(2)}) collective-permute-start(bf16[32,1024]{1,0:T(8,128)(2,1)S(1)} %bitcast.115), channel_id=1, source_target_pairs={{0,2},{2,0},{1,3},{3,1},{4,6},{6,4},{5,7},{7,5},{8,10},{10,8},{9,1... | collective-permute-start | bytes 196616 | tf_op jit(solution)/shard_map/ppermute | solution.py:238
  11.5 10.5 %collective-permute-start.3 = (bf16[2,32,1024]{2,1,0:T(8,128)(2,1)S(1)}, bf16[2,32,1024]{2,1,0:T(8,128)(2,1)S(1)}, u32[]{:S(2)}, u32[]{:S(2)}) collective-permute-start(bf16[2,32,1024]{2,1,0:T(8,128)(2,1)S(1)} %maximum_select_fusion.2), channel_id=1, source_target_pairs={{0,4},{4,8},{8,12},{12,0},{1,5},{5,9},{9,13},{13,1},{2,6},{6,10},{... | collective-permute-start | bytes 393224 | tf_op jit(solution)/shard_map/ppermute | solution.py:240
  13.1 9.0 %collective-permute-start.1 = (bf16[2,32,1024]{2,1,0:T(8,128)(2,1)S(1)}, bf16[2,32,1024]{2,1,0:T(8,128)(2,1)S(1)}, u32[]{:S(2)}, u32[]{:S(2)}) collective-permute-start(bf16[2,32,1024]{2,1,0:T(8,128)(2,1)S(1)} %maximum_select_fusion.2), channel_id=1, source_target_pairs={{0,12},{4,0},{8,4},{12,8},{1,13},{5,1},{9,5},{13,9},{2,14},{6,2},{... | collective-permute-start | bytes 393224 | tf_op jit(solution)/shard_map/ppermute | solution.py:240
  14.8 7.2 %collective-permute-start.2 = (bf16[2,32,1024]{2,1,0:T(8,128)(2,1)S(1)}, bf16[2,32,1024]{2,1,0:T(8,128)(2,1)S(1)}, u32[]{:S(2)}, u32[]{:S(2)}) collective-permute-start(bf16[2,32,1024]{2,1,0:T(8,128)(2,1)S(1)} %maximum_select_fusion.2), channel_id=1, source_target_pairs={{0,8},{4,12},{8,0},{12,4},{1,9},{5,13},{9,1},{13,5},{2,10},{6,14},... | collective-permute-start | bytes 393224 | tf_op jit(solution)/shard_map/ppermute | solution.py:240
  21.3 16.8 %collective-permute-start.18 = (f16[4,136,1024]{2,1,0:T(8,128)(2,1)S(1)}, f16[4,136,1024]{2,1,0:T(8,128)(2,1)S(1)}, u32[]{:S(2)}, u32[]{:S(2)}) collective-permute-start(f16[4,136,1024]{2,1,0:T(8,128)(2,1)S(1)} %bitcast.112), channel_id=1, source_target_pairs={{0,4},{1,13},{4,8},{5,1},{8,12},{9,5},{12,0},{13,9},{2,6},{3,15},{... | collective-permute-start | bytes 3342344 | tf_op jit(solution)/shard_map/ppermute | solution.py:163
  22.1 10.8 %collective-permute-start.4 = (bf16[4,2,32,1024]{3,2,1,0:T(8,128)(2,1)S(1)}, bf16[4,2,32,1024]{3,2,1,0:T(8,128)(2,1)S(1)}, u32[]{:S(2)}, u32[]{:S(2)}) collective-permute-start(bf16[4,2,32,1024]{3,2,1,0:T(8,128)(2,1)S(1)} %get-tuple-element.42), channel_id=1, source_target_pairs={{0,1},{1,0},{2,3},{3,2},{4,5},{5,4},{6,7},{7,6},{8,9},{9,8},{10,11... | collective-permute-start | bytes 1572872 | tf_op jit(solution)/shard_map/ppermute | solution.py:242
  29.1 2.8 %copy-start.4 = (f32[1632,1024]{1,0:T(8,128)}, f32[1632,1024]{1,0:T(8,128)S(1)}, u32[]{:S(2)}) copy-start(f32[1632,1024]{1,0:T(8,128)S(1)} %shard_map.98) | copy-start | bytes 20054020
  31.9 18.3 %collective-permute-start.15 = (f16[4,136,1024]{2,1,0:T(8,128)(2,1)S(1)}, f16[4,136,1024]{2,1,0:T(8,128)(2,1)}, u32[]{:S(2)}, u32[]{:S(2)}) collective-permute-start(f16[4,136,1024]{2,1,0:T(8,128)(2,1)S(1)} %bitcast.113), channel_id=1, source_target_pairs={{0,4},{1,13},{4,8},{5,1},{8,12},{9,5},{12,0},{13,9},{2,6},{3,15},{... | collective-permute-start | bytes 3342344 | tf_op jit(solution)/shard_map/ppermute | solution.py:169
  33.2 18.9 %collective-permute-start.5 = (bf16[512,1024]{1,0:T(8,128)(2,1)S(1)}, bf16[512,1024]{1,0:T(8,128)(2,1)S(1)}, u32[]{:S(2)}, u32[]{:S(2)}) collective-permute-start(bf16[512,1024]{1,0:T(8,128)(2,1)S(1)} %bitcast.106), channel_id=1, source_target_pairs={{0,16},{1,113},{16,32},{17,1},{32,48},{33,17},{48,64},{49,33},{64,... | collective-permute-start | bytes 3145736 | tf_op jit(solution)/shard_map/ppermute | solution.py:247
  39.7 29.2 %collective-permute-start.19 = (f16[4,136,1024]{2,1,0:T(8,128)(2,1)}, f16[4,136,1024]{2,1,0:T(8,128)(2,1)}, u32[]{:S(2)}, u32[]{:S(2)}) collective-permute-start(f16[4,136,1024]{2,1,0:T(8,128)(2,1)} %select_convert_fusion), channel_id=1, source_target_pairs={{0,4},{1,13},{4,8},{5,1},{8,12},{9,5},{12,0},{13,9},{2,6},{3,15},{... | collective-permute-start | bytes 3342344 | tf_op jit(solution)/shard_map/ppermute | solution.py:171
  50.2 19.8 %collective-permute-start.16 = (f16[4,136,1024]{2,1,0:T(8,128)(2,1)}, f16[4,136,1024]{2,1,0:T(8,128)(2,1)}, u32[]{:S(2)}, u32[]{:S(2)}) collective-permute-start(f16[4,136,1024]{2,1,0:T(8,128)(2,1)} %collective-permute-done.15), channel_id=1, source_target_pairs={{0,1},{1,0},{2,3},{3,2},{4,5},{5,4},{6,7},{7,6},{8,9},{9,8},{10,11... | collective-permute-start | bytes 3342344 | tf_op jit(solution)/shard_map/ppermute | solution.py:170
  52.1 16.8 %collective-permute-start.6 = (bf16[512,1024]{1,0:T(8,128)(2,1)S(1)}, bf16[512,1024]{1,0:T(8,128)(2,1)}, u32[]{:S(2)}, u32[]{:S(2)}) collective-permute-start(bf16[512,1024]{1,0:T(8,128)(2,1)S(1)} %collective-permute-done.5.refs_2_), channel_id=1, source_target_pairs={{0,16},{1,113},{16,32},{17,1},{32,48},{33,17},{48,64},{49,33},{64,... | collective-permute-start | bytes 3145736 | tf_op jit(solution)/shard_map/ppermute | solution.py:247
  52.1 65.2 %collective-permute-start.26 = (f32[131072]{0:T(1024)}, f32[131072]{0:T(1024)}, u32[]{:S(2)}, u32[]{:S(2)}) collective-permute-start(f32[131072]{0:T(1024)} %bitcast.66), channel_id=1, source_target_pairs={{0,128},{128,0},{1,129},{129,1},{2,130},{130,2},{3,131},{131,3},{4... | collective-permute-start | bytes 1572872 | tf_op jit(solution)/shard_map/ppermute | solution.py:261
  54.4 66.0 %collective-permute-start.12 = (bf16[512,1024]{1,0:T(8,128)(2,1)S(1)}, bf16[512,1024]{1,0:T(8,128)(2,1)S(1)}, u32[]{:S(2)}, u32[]{:S(2)}) collective-permute-start(bf16[512,1024]{1,0:T(8,128)(2,1)S(1)} %collective-permute-done.5.refs_2_), channel_id=1, source_target_pairs={{0,1},{1,0},{2,3},{3,2},{4,5},{5,4},{6,7},{7,6},{8,9},{9,8},{10,11... | collective-permute-start | bytes 3145736 | tf_op jit(solution)/shard_map/ppermute | solution.py:249
  68.9 55.9 %collective-permute-start.11 = (bf16[512,1024]{1,0:T(8,128)(2,1)}, bf16[512,1024]{1,0:T(8,128)(2,1)S(1)}, u32[]{:S(2)}, u32[]{:S(2)}) collective-permute-start(bf16[512,1024]{1,0:T(8,128)(2,1)} %collective-permute-done.6.refs_1_), channel_id=1, source_target_pairs={{0,1},{1,0},{2,3},{3,2},{4,5},{5,4},{6,7},{7,6},{8,9},{9,8},{10,11... | collective-permute-start | bytes 3145736 | tf_op jit(solution)/shard_map/ppermute | solution.py:249
  68.9 39.7 %collective-permute-start.7 = (bf16[512,1024]{1,0:T(8,128)(2,1)}, bf16[512,1024]{1,0:T(8,128)(2,1)S(1)}, u32[]{:S(2)}, u32[]{:S(2)}) collective-permute-start(bf16[512,1024]{1,0:T(8,128)(2,1)} %collective-permute-done.6.refs_1_), channel_id=1, source_target_pairs={{0,16},{1,113},{16,32},{17,1},{32,48},{33,17},{48,64},{49,33},{64,... | collective-permute-start | bytes 3145736 | tf_op jit(solution)/shard_map/ppermute | solution.py:247
  73.0 15.1 %collective-permute-start.20 = (f16[1,136,1024]{2,1,0:T(8,128)(2,1)S(1)}, f16[1,136,1024]{2,1,0:T(8,128)(2,1)S(1)}, u32[]{:S(2)}, u32[]{:S(2)}) collective-permute-start(f16[1,136,1024]{2,1,0:T(8,128)(2,1)S(1)} %fusion.10), channel_id=1, source_target_pairs={{0,16},{1,113},{16,32},{17,1},{32,48},{33,17},{48,64},{49,33},{64,... | collective-permute-start | bytes 835592 | tf_op jit(solution)/shard_map/ppermute | solution.py:176
  91.2 7.8 %collective-permute-start.21 = (f16[1,136,1024]{2,1,0:T(8,128)(2,1)S(1)}, f16[1,136,1024]{2,1,0:T(8,128)(2,1)S(1)}, u32[]{:S(2)}, u32[]{:S(2)}) collective-permute-start(f16[1,136,1024]{2,1,0:T(8,128)(2,1)S(1)} %fusion.7), channel_id=1, source_target_pairs={{0,16},{1,113},{16,32},{17,1},{32,48},{33,17},{48,64},{49,33},{64,... | collective-permute-start | bytes 835592 | tf_op jit(solution)/shard_map/ppermute | solution.py:176
  99.1 15.1 %collective-permute-start.23 = (f16[1,136,1024]{2,1,0:T(8,128)(2,1)S(1)}, f16[1,136,1024]{2,1,0:T(8,128)(2,1)S(1)}, u32[]{:S(2)}, u32[]{:S(2)}) collective-permute-start(f16[1,136,1024]{2,1,0:T(8,128)(2,1)S(1)} %get-tuple-element.14), channel_id=1, source_target_pairs={{0,64},{16,80},{32,96},{48,112},{64,0},{80,16},{96,32},{112,48},{2... | collective-permute-start | bytes 835592 | tf_op jit(solution)/shard_map/ppermute | solution.py:181
  108.7 8.4 %collective-permute-start.22 = (f16[1,136,1024]{2,1,0:T(8,128)(2,1)S(1)}, f16[1,136,1024]{2,1,0:T(8,128)(2,1)S(1)}, u32[]{:S(2)}, u32[]{:S(2)}) collective-permute-start(f16[1,136,1024]{2,1,0:T(8,128)(2,1)S(1)} %fusion.3), channel_id=1, source_target_pairs={{0,16},{1,113},{16,32},{17,1},{32,48},{33,17},{48,64},{49,33},{64,... | collective-permute-start | bytes 835592 | tf_op jit(solution)/shard_map/ppermute | solution.py:176
  108.8 9.3 %copy-start.5 = (f32[131072]{0:T(1024)S(1)}, f32[131072]{0:T(1024)}, u32[]{:S(2)}) copy-start(f32[131072]{0:T(1024)} %param.9) | copy-start | bytes 1572868
  108.8 9.3 %copy-start.6 = (f32[131072]{0:T(1024)S(1)}, f32[131072]{0:T(1024)}, u32[]{:S(2)}) copy-start(f32[131072]{0:T(1024)} %param.11) | copy-start | bytes 1572868
  114.1 10.7 %collective-permute-start.8 = (bf16[256,1024]{1,0:T(8,128)(2,1)S(1)}, bf16[256,1024]{1,0:T(8,128)(2,1)S(1)}, u32[]{:S(2)}, u32[]{:S(2)}) collective-permute-start(bf16[256,1024]{1,0:T(8,128)(2,1)S(1)} %constant_dynamic-slice_fusion), channel_id=1, source_target_pairs={{0,16},{1,113},{16,32},{17,1},{32,48},{33,17},{48,64},{49,33},{64,... | collective-permute-start | bytes 1572872 | tf_op jit(solution)/shard_map/ppermute | solution.py:250
  117.1 13.6 %collective-permute-start.10 = (bf16[512,1024]{1,0:T(8,128)(2,1)S(1)}, bf16[512,1024]{1,0:T(8,128)(2,1)S(1)}, u32[]{:S(2)}, u32[]{:S(2)}) collective-permute-start(bf16[512,1024]{1,0:T(8,128)(2,1)S(1)} %collective-permute-done.7.refs_1_), channel_id=1, source_target_pairs={{0,1},{1,0},{2,3},{3,2},{4,5},{5,4},{6,7},{7,6},{8,9},{9,8},{10,11... | collective-permute-start | bytes 3145736 | tf_op jit(solution)/shard_map/ppermute | solution.py:249
  117.3 11.8 %collective-permute-start.24 = (f32[2,32,1024]{2,1,0:T(8,128)S(1)}, f32[2,32,1024]{2,1,0:T(8,128)S(1)}, u32[]{:S(2)}, u32[]{:S(2)}) collective-permute-start(f32[2,32,1024]{2,1,0:T(8,128)S(1)} %dynamic-slice_bitcast_fusion), channel_id=1, source_target_pairs={{0,1},{1,0},{2,3},{3,2},{4,5},{5,4},{6,7},{7,6},{8,9},{9,8},{10,11... | collective-permute-start | bytes 786440 | tf_op jit(solution)/shard_map/ppermute | solution.py:186
  124.8 8.8 %collective-permute-start.9 = (bf16[256,1024]{1,0:T(8,128)(2,1)S(1)}, bf16[256,1024]{1,0:T(8,128)(2,1)S(1)}, u32[]{:S(2)}, u32[]{:S(2)}) collective-permute-start(bf16[256,1024]{1,0:T(8,128)(2,1)S(1)} %collective-permute-done.8.refs_1_), channel_id=1, source_target_pairs={{0,1},{1,0},{2,3},{3,2},{4,5},{5,4},{6,7},{7,6},{8,9},{9,8},{10,11... | collective-permute-start | bytes 1572872 | tf_op jit(solution)/shard_map/ppermute | solution.py:251
  129.1 6.6 %collective-permute-start.25 = (f32[32,1024]{1,0:T(8,128)S(1)}, f32[32,1024]{1,0:T(8,128)S(1)}, u32[]{:S(2)}, u32[]{:S(2)}) collective-permute-start(f32[32,1024]{1,0:T(8,128)S(1)} %dynamic-slice_bitcast_fusion.1), channel_id=1, source_target_pairs={{0,2},{2,0},{1,3},{3,1},{4,6},{6,4},{5,7},{7,5},{8,10},{10,8},{9,1... | collective-permute-start | bytes 393224 | tf_op jit(solution)/shard_map/ppermute | solution.py:187
  (3 other events, 5.2 us)
